TPU v7x, 128 devices: a whole 4x4x4 slice. The times are simulated.
128 devices in a mesh: gx: 4 (over x), gy: 4 (over y), gz: 8 (over z, core).
Axes of the slice: x: 4, y: 4, z: 4, core: 2. Of those that a mesh axis runs over, the one named last changes fastest.
Arguments:
- seg_rows: bfloat16 [16384, 128, 128], P(('gx', 'gy', 'gz')), may hold values from -6 to 6
- owner_map: int32 [16384, 1], replicated, may hold values from 0 to 127; in each aligned block of 128 rows (0 to 127, 128 to 255, ...) at most 2 rows name the same one
- ghost_pick: int32 [128, 1], P(('gx', 'gy', 'gz')), may hold values from 0 to 127
- slab_cost: int32 [4, 4, 8, 3, 1024], P('gx', 'gy', 'gz'), may hold values from 1 to 24
Outputs:
- forces: bfloat16 [128, 128, 2, 128, 128], P(('gx', 'gy', 'gz'))
- cut_points: float32 [7], replicated
Inputs may be any that keep to these rules, and one draw needn't show every extreme that they name: `owner_map`: among the 128 blocks of one device (aligned runs of 128 rows) no owner is named more than 2 times; some device names some owner exactly 2 times.
All inputs are finite; a program needn't handle non-finite values.
Results may differ from a plain program's by a relative error of at most 0.0034.
Values may be sent and summed in bfloat16 or wider, within the bound.
No kernel may reach another device: no remote copies, remote signals or barrier semaphores. Data moves between devices by JAX's collectives and lax.ppermute only.
A program may use at most 128 MiB of HBM per device.

v0:
```python
import functools
import math

import jax
import jax.numpy as jnp
from jax import lax
from jax.sharding import Mesh
from jax.sharding import PartitionSpec as P

GZ = ("gz_0", "gz_1")
GX_GY_GZ = ("gx", "gy", "gz_0", "gz_1")


sharpness = 8.0
force_gain = 2.0
radius_eps = 0.001


def over_axes(shard, axes):
    return functools.reduce(lax.psum, axes, shard)


def padded_2(cells, sides, width):
    for axis, dim in sides:
        count = lax.axis_size(axis)
        head = lax.slice_in_dim(cells, 0, width, axis=dim)
        tail = lax.slice_in_dim(cells, cells.shape[dim] - width, cells.shape[dim], axis=dim)
        cells = jnp.concatenate(
            [
                lax.ppermute(tail, axis, [(i, (i + 1) % count) for i in range(count)]),
                cells,
                lax.ppermute(head, axis, [((i + 1) % count, i) for i in range(count)]),
            ],
            axis=dim,
        )
    return cells


def exchange_in_groups(shard, axis, split_dim, concat_dim, work, item_dim, out_dim):
    items = jax.tree.leaves(shard)[0].shape[item_dim]
    count = 2 if items % 2 == 0 else 1
    done = []
    for k in range(count):
        group = jax.tree.map(
            lambda a: lax.slice_in_dim(
                a, k * (items // count), (k + 1) * (items // count), axis=item_dim
            ),
            shard,
        )
        done.append(
            work(
                lax.all_to_all(
                    group, axis, split_axis=split_dim, concat_axis=concat_dim, tiled=True
                )
            )
        )
    return jax.tree.map(lambda *parts: jnp.concatenate(parts, axis=out_dim), *done)


def bisect_cuts(histogram):
    running = jnp.cumsum(histogram, axis=1, dtype=jnp.int32)
    total_cost = running[:, -1]
    below = (2 * running < total_cost[:, None]).astype(jnp.int32)
    position = jnp.sum(below, axis=1, dtype=jnp.int32)
    before = jnp.sum(histogram * below, axis=1, dtype=jnp.int32)
    bins_index = lax.broadcasted_iota(jnp.int32, histogram.shape, 1)
    at_cut = jnp.sum(
        jnp.where(bins_index == position[:, None], histogram, 0), axis=1, dtype=jnp.int32
    )
    remain = (total_cost - 2 * before).astype(jnp.float32)
    return (
        position.astype(jnp.float32) + remain / (2 * at_cut).astype(jnp.float32)
    ) / histogram.shape[1]


def kernel_weights(left_sq, right_sq, inner):
    spread = left_sq + right_sq - 2.0 * inner
    return jnp.exp(-sharpness * spread / (left_sq + right_sq + radius_eps)).astype(jnp.bfloat16)


def pair_forces(slot_rows, ghost_set, ghost_sq):
    rows_f = slot_rows.astype(jnp.float32)
    own_sq = jnp.sum(rows_f * rows_f, axis=-1)
    own_inner = jnp.einsum("sbw,scw->sbc", slot_rows, slot_rows, preferred_element_type=jnp.float32)
    ghost_inner = jnp.einsum(
        "sbw,mw->sbm", slot_rows, ghost_set, preferred_element_type=jnp.float32
    )
    own_kernel = kernel_weights(own_sq[:, :, None], own_sq[:, None, :], own_inner)
    ghost_kernel = kernel_weights(own_sq[:, :, None], ghost_sq[None, None, :], ghost_inner)
    weight_sum = jnp.sum(own_kernel.astype(jnp.float32), axis=-1) + jnp.sum(
        ghost_kernel.astype(jnp.float32), axis=-1
    )
    pulled = jnp.einsum("sbc,scw->sbw", own_kernel, slot_rows, preferred_element_type=jnp.float32)
    pulled = pulled + jnp.einsum(
        "sbm,mw->sbw", ghost_kernel, ghost_set, preferred_element_type=jnp.float32
    )
    return (force_gain * (pulled - weight_sum[..., None] * rows_f)).astype(jnp.bfloat16)


def per_device(seg_rows, owner_map, ghost_pick, slab_cost):
    count_x = lax.axis_size("gx")
    count_y = lax.axis_size("gy")
    count_z = lax.axis_size(GZ)
    device_count = count_x * count_y * count_z
    blocks_here, block_rows, width = seg_rows.shape
    capacity = max(2, (2 * blocks_here + device_count - 1) // device_count)
    own_index = lax.axis_index(GX_GY_GZ)
    index_x = lax.axis_index("gx")
    index_y = lax.axis_index("gy")
    local_cost = slab_cost[0, 0, 0]
    bins_count = local_cost.shape[1]
    half_part = index_x // (count_x // 2)
    quarter = half_part * 2 + index_y // (count_y // 2)
    x_term = local_cost[0][None]
    y_term = jnp.where(
        lax.broadcasted_iota(jnp.int32, (2, bins_count), 0) == half_part, local_cost[1][None], 0
    )
    z_term = jnp.where(
        lax.broadcasted_iota(jnp.int32, (4, bins_count), 0) == quarter, local_cost[2][None], 0
    )
    hist_x = over_axes(x_term, GX_GY_GZ)
    hist_y = over_axes(y_term, GX_GY_GZ)
    hist_z = over_axes(z_term, GX_GY_GZ)
    histogram = jnp.concatenate([hist_x, hist_y, hist_z], axis=0)
    extent = jnp.array([count_x, count_y, count_y, count_z, count_z, count_z, count_z], jnp.float32)
    cut_points = bisect_cuts(histogram) * extent
    exported = jnp.take(seg_rows, ghost_pick[0], axis=0)
    padded = padded_2(exported[None, None, None], (("gx", 0), ("gy", 1), (GZ, 2)), 1)
    ghost_set = jnp.concatenate(
        [
            padded[0, 1, 1],
            padded[2, 1, 1],
            padded[1, 0, 1],
            padded[1, 2, 1],
            padded[1, 1, 0],
            padded[1, 1, 2],
        ],
        axis=0,
    ).reshape(-1, width)
    ghost_float = ghost_set.astype(jnp.float32)
    ghost_sq = jnp.sum(ghost_float * ghost_float, axis=-1)
    all_owners = owner_map[:, 0].reshape(device_count, blocks_here)
    own_owners = lax.dynamic_index_in_dim(all_owners, own_index, 0, keepdims=False)
    block_order = lax.broadcasted_iota(jnp.int32, (blocks_here,), 0)
    earlier = block_order[:, None] < block_order[None, :]
    same_owner = own_owners[:, None] == own_owners[None, :]
    slot_rank = jnp.sum((same_owner & earlier).astype(jnp.int32), axis=0, dtype=jnp.int32)
    slot_of = own_owners * capacity + slot_rank
    slot_ids = lax.broadcasted_iota(jnp.int32, (device_count * capacity,), 0)
    matches = slot_of[None, :] == slot_ids[:, None]
    source_block = jnp.sum(jnp.where(matches, block_order[None, :], 0), axis=1, dtype=jnp.int32)
    filled = jnp.any(matches, axis=1)
    outgoing = jnp.where(
        filled[:, None, None], jnp.take(seg_rows, source_block, axis=0), jnp.zeros((), jnp.bfloat16)
    )
    outgoing = outgoing.reshape(device_count, capacity, block_rows, width)
    arrivals = jnp.sum((all_owners == own_index).astype(jnp.int32), axis=1, dtype=jnp.int32)
    valid_slot = lax.broadcasted_iota(jnp.int32, (device_count, capacity), 1) < arrivals[:, None]

    def settle(received):
        flat_slots = received.reshape(-1, block_rows, width)
        slot_total = flat_slots.shape[0]
        group_size = math.gcd(slot_total, 16)
        grouped = flat_slots.reshape(slot_total // group_size, group_size, block_rows, width)
        settled = lax.map(lambda piece: pair_forces(piece, ghost_set, ghost_sq), grouped)
        return settled.reshape(received.shape)

    forces = exchange_in_groups(outgoing, GX_GY_GZ, 0, 0, settle, 1, 1)
    forces = jnp.where(valid_slot[:, :, None, None], forces, jnp.zeros((), jnp.bfloat16))
    return (forces[None], cut_points)


def solution(mesh):
    finer = Mesh(
        mesh.devices.reshape(mesh.shape["gx"], mesh.shape["gy"], 4, 2), ("gx", "gy", "gz_0", "gz_1")
    )
    in_specs = (P(GX_GY_GZ, None, None), P(), P(GX_GY_GZ, None), P("gx", "gy", GZ, None, None))
    out_specs = (P(GX_GY_GZ, None, None, None, None), P())
    return jax.shard_map(
        per_device, mesh=finer, in_specs=in_specs, out_specs=out_specs, check_vma=False
    )
```

profile of v0, /device:TPU:1, one launch (start us, length us, event | category | flops | bytes accessed | tf_op | source)
XLA Modules:
  0.0 347.4 jit_solution(9996375845349677162)
XLA Ops:
  2.7 10.8 %gather_fusion = bf16[256,128,128]{2,1,0:T(8,128)(2,1)} fusion(bf16[128,128,128]{2,1,0:T(8,128)(2,1)} %param.9, s32[1024]{0:T(1024)S(1)} %pad_clamp_fusion), kind=kCustom, calls=%fused_computation | custom fusion | bytes 16778240 | tf_op jit(solution)/shard_map/jit(_take)/gather | solution.py:154
  13.5 4.6 %select_select_fusion = bf16[128,2,128,128]{3,2,1,0:T(8,128)(2,1)S(1)} fusion(bf16[128,2,128,128]{3,2,1,0:T(8,128)(2,1)} %bitcast.162, pred[128,2]{1,0:T(8,128)(4,1)S(1)} %compare_and_fusion, pred[128,2]{1,0:T(8,128)(4,1)S(1)} %broadcast_in_dim.123), kind=kLoop, calls=%fused_computation.74 | loop fusion | flops 8388608 | bytes 16777728 | tf_op jit(solution)/shard_map/jit(_where)/select_n | solution.py:153
  18.2 3.9 %fusion.63 = (bf16[128,1,128,128]{3,2,1,0:T(8,128)(2,1)}, bf16[128,1,128,128]{3,2,1,0:T(8,128)(2,1)}) fusion(bf16[128,2,128,128]{3,2,1,0:T(8,128)(2,1)S(1)} %select_select_fusion), kind=kLoop, calls=%fused_computation.126 | loop fusion | bytes 16777216 | tf_op jit(solution)/shard_map/slice | solution.py:45
  22.1 11.9 %all-to-all-start = ((bf16[128,1,128,128]{3,2,1,0:T(8,128)(2,1)}), bf16[128,1,128,128]{3,2,1,0:T(8,128)(2,1)}, u32[]{:S(2)}, u32[]{:S(2)}) async-start(bf16[128,1,128,128]{3,2,1,0:T(8,128)(2,1)} %get-tuple-element.111), calls=%async_computation | async-start | bytes 8388608 | tf_op jit(solution)/shard_map/all_to_all | solution.py:52
  38.3 50.5 %all-reduce.2 = (s32[4,1024]{1,0:T(4,128)S(1)}, s32[2,1024]{1,0:T(2,128)S(1)}, s32[1,1024]{1,0:T(1,128)S(1)}) all-reduce(s32[4,1024]{1,0:T(4,128)S(1)} %broadcast_select_fusion, s32[2,1024]{1,0:T(2,128)S(1)} %broadcast_select_fusion.1, s32[1,1024]{1,0:T(1,128)S(1)} %get-tuple-element.113), channel_id=1, replica_groups=mesh['gx'=4,'gy'=4,'gz_0'=4,'gz_1'=2] {'gx'}, use_global_device_ids=true, to_apply=%region_23.24 | all-reduce | flops 7168 | bytes 57344 | tf_op jit(solution)/shard_map/psum | solution.py:20
  88.8 13.3 %all-reduce.1 = (s32[4,1024]{1,0:T(4,128)S(1)}, s32[2,1024]{1,0:T(2,128)S(1)}, s32[1,1024]{1,0:T(1,128)S(1)}) all-reduce(s32[4,1024]{1,0:T(4,128)S(1)} %get-tuple-element.97, s32[2,1024]{1,0:T(2,128)S(1)} %get-tuple-element.98, s32[1,1024]{1,0:T(1,128)S(1)} %get-tuple-element.99), channel_id=1, replica_groups=mesh['gx'=4,'gy'=4,'gz_0'=4,'gz_1'=2] {'gy'}, use_global_device_ids=true, to_apply=%region_24.25 | all-reduce | flops 7168 | bytes 57344 | tf_op jit(solution)/shard_map/psum | solution.py:20
  102.1 13.6 %all-reduce = (s32[4,1024]{1,0:T(4,128)S(1)}, s32[2,1024]{1,0:T(2,128)S(1)}, s32[1,1024]{1,0:T(1,128)S(1)}) all-reduce(s32[4,1024]{1,0:T(4,128)S(1)} %get-tuple-element.94, s32[2,1024]{1,0:T(2,128)S(1)} %get-tuple-element.95, s32[1,1024]{1,0:T(1,128)S(1)} %get-tuple-element.96), channel_id=1, replica_groups=mesh['gx'=4,'gy'=4,'gz_0'=4,'gz_1'=2] {'gz_0'}, use_global_device_ids=true, to_apply=%region_25.26 | all-reduce | flops 7168 | bytes 57344 | tf_op jit(solution)/shard_map/psum | solution.py:20
  115.7 14.2 %all-reduce.3 = (s32[4,1024]{1,0:T(4,128)S(1)}, s32[2,1024]{1,0:T(2,128)S(1)}, s32[1,1024]{1,0:T(1,128)S(1)}) all-reduce(s32[4,1024]{1,0:T(4,128)S(1)} %get-tuple-element.91, s32[2,1024]{1,0:T(2,128)S(1)} %get-tuple-element.92, s32[1,1024]{1,0:T(1,128)S(1)} %get-tuple-element.93), channel_id=1, replica_groups=mesh['gx'=4,'gy'=4,'gz_0'=4,'gz_1'=2] {'gz_1'}, use_global_device_ids=true, to_apply=%region_26.27 | all-reduce | flops 7168 | bytes 57344 | tf_op jit(solution)/shard_map/psum | solution.py:20
  146.4 9.5 %all-to-all-start.1 = ((bf16[128,1,128,128]{3,2,1,0:T(8,128)(2,1)}), bf16[128,1,128,128]{3,2,1,0:T(8,128)(2,1)}, u32[]{:S(2)}, u32[]{:S(2)}) async-start(bf16[128,1,128,128]{3,2,1,0:T(8,128)(2,1)} %get-tuple-element.112), calls=%async_computation.1 | async-start | bytes 8388608 | tf_op jit(solution)/shard_map/all_to_all | solution.py:52
  155.9 3.0 broadcast.163.clone.1
  158.9 89.1 %while.21 = (s32[]{:T(128)}, bf16[8,16,128,128]{3,2,1,0:T(8,128)(2,1)}, bf16[8,16,128,128]{3,2,1,0:T(8,128)(2,1)}, f32[768]{0:T(1024)S(1)}, bf16[768,128]{1,0:T(8,128)(2,1)S(1)}, /*index=5*/s32[]{:T(128)}) while((s32[]{:T(128)}, bf16[8,16,128,128]{3,2,1,0:T(8,128)(2,1)}, bf16[8,16,128,128]{3,2,1,0:T(8,128)(2,1)}, f32[768]{0:T(1024)S(1)}, ...), condition=%wide.region_9.10_spmd, body=%wide.region_5.9_spmd.sunk | while | flops 958394368 | bytes 13063241 | solution.py:165
  160.3 3.5 %convert_reduce_fusion.12 = (f32[16,128]{1,0:T(8,128)S(1)}, bf16[16,128,768]{2,1,0:T(8,128)(2,1)S(1)}) fusion(bf16[768,128]{1,0:T(8,128)(2,1)S(1)} %get-tuple-element.228, bf16[8,16,128,128]{3,2,1,0:T(8,128)(2,1)} %get-tuple-element.226, s32[]{:T(128)} %get-tuple-element.218, f32[768]{0:T(1024)S(1)} %get-tuple-element.227, f32[16,128]{1,0:T(8,128)S(1)} %fusion.86), kind=kOutput, calls=%fused_computation.6.clone.1 | convolution fusion | flops 416806912 | bytes 3886592 | tf_op jit(solution)/shard_map/while/body/eval_jaxpr/sbw,mw->sbm/dot_general | solution.py:85
  167.1 2.9 fusion.88
  171.4 3.5 %convert_reduce_fusion.12 = (f32[16,128]{1,0:T(8,128)S(1)}, bf16[16,128,768]{2,1,0:T(8,128)(2,1)S(1)}) fusion(bf16[768,128]{1,0:T(8,128)(2,1)S(1)} %get-tuple-element.228, bf16[8,16,128,128]{3,2,1,0:T(8,128)(2,1)} %get-tuple-element.226, s32[]{:T(128)} %get-tuple-element.218, f32[768]{0:T(1024)S(1)} %get-tuple-element.227, f32[16,128]{1,0:T(8,128)S(1)} %fusion.86), kind=kOutput, calls=%fused_computation.6.clone.1 | convolution fusion | flops 416806912 | bytes 3886592 | tf_op jit(solution)/shard_map/while/body/eval_jaxpr/sbw,mw->sbm/dot_general | solution.py:85
  178.3 2.9 fusion.88
  182.7 3.5 %convert_reduce_fusion.12 = (f32[16,128]{1,0:T(8,128)S(1)}, bf16[16,128,768]{2,1,0:T(8,128)(2,1)S(1)}) fusion(bf16[768,128]{1,0:T(8,128)(2,1)S(1)} %get-tuple-element.228, bf16[8,16,128,128]{3,2,1,0:T(8,128)(2,1)} %get-tuple-element.226, s32[]{:T(128)} %get-tuple-element.218, f32[768]{0:T(1024)S(1)} %get-tuple-element.227, f32[16,128]{1,0:T(8,128)S(1)} %fusion.86), kind=kOutput, calls=%fused_computation.6.clone.1 | convolution fusion | flops 416806912 | bytes 3886592 | tf_op jit(solution)/shard_map/while/body/eval_jaxpr/sbw,mw->sbm/dot_general | solution.py:85
  193.8 3.5 %convert_reduce_fusion.12 = (f32[16,128]{1,0:T(8,128)S(1)}, bf16[16,128,768]{2,1,0:T(8,128)(2,1)S(1)}) fusion(bf16[768,128]{1,0:T(8,128)(2,1)S(1)} %get-tuple-element.228, bf16[8,16,128,128]{3,2,1,0:T(8,128)(2,1)} %get-tuple-element.226, s32[]{:T(128)} %get-tuple-element.218, f32[768]{0:T(1024)S(1)} %get-tuple-element.227, f32[16,128]{1,0:T(8,128)S(1)} %fusion.86), kind=kOutput, calls=%fused_computation.6.clone.1 | convolution fusion | flops 416806912 | bytes 3886592 | tf_op jit(solution)/shard_map/while/body/eval_jaxpr/sbw,mw->sbm/dot_general | solution.py:85
  204.9 3.5 %convert_reduce_fusion.12 = (f32[16,128]{1,0:T(8,128)S(1)}, bf16[16,128,768]{2,1,0:T(8,128)(2,1)S(1)}) fusion(bf16[768,128]{1,0:T(8,128)(2,1)S(1)} %get-tuple-element.228, bf16[8,16,128,128]{3,2,1,0:T(8,128)(2,1)} %get-tuple-element.226, s32[]{:T(128)} %get-tuple-element.218, f32[768]{0:T(1024)S(1)} %get-tuple-element.227, f32[16,128]{1,0:T(8,128)S(1)} %fusion.86), kind=kOutput, calls=%fused_computation.6.clone.1 | convolution fusion | flops 416806912 | bytes 3886592 | tf_op jit(solution)/shard_map/while/body/eval_jaxpr/sbw,mw->sbm/dot_general | solution.py:85
  216.0 3.5 %convert_reduce_fusion.12 = (f32[16,128]{1,0:T(8,128)S(1)}, bf16[16,128,768]{2,1,0:T(8,128)(2,1)S(1)}) fusion(bf16[768,128]{1,0:T(8,128)(2,1)S(1)} %get-tuple-element.228, bf16[8,16,128,128]{3,2,1,0:T(8,128)(2,1)} %get-tuple-element.226, s32[]{:T(128)} %get-tuple-element.218, f32[768]{0:T(1024)S(1)} %get-tuple-element.227, f32[16,128]{1,0:T(8,128)S(1)} %fusion.86), kind=kOutput, calls=%fused_computation.6.clone.1 | convolution fusion | flops 416806912 | bytes 3886592 | tf_op jit(solution)/shard_map/while/body/eval_jaxpr/sbw,mw->sbm/dot_general | solution.py:85
  227.2 3.5 %convert_reduce_fusion.12 = (f32[16,128]{1,0:T(8,128)S(1)}, bf16[16,128,768]{2,1,0:T(8,128)(2,1)S(1)}) fusion(bf16[768,128]{1,0:T(8,128)(2,1)S(1)} %get-tuple-element.228, bf16[8,16,128,128]{3,2,1,0:T(8,128)(2,1)} %get-tuple-element.226, s32[]{:T(128)} %get-tuple-element.218, f32[768]{0:T(1024)S(1)} %get-tuple-element.227, f32[16,128]{1,0:T(8,128)S(1)} %fusion.86), kind=kOutput, calls=%fused_computation.6.clone.1 | convolution fusion | flops 416806912 | bytes 3886592 | tf_op jit(solution)/shard_map/while/body/eval_jaxpr/sbw,mw->sbm/dot_general | solution.py:85
  238.3 3.5 %convert_reduce_fusion.12 = (f32[16,128]{1,0:T(8,128)S(1)}, bf16[16,128,768]{2,1,0:T(8,128)(2,1)S(1)}) fusion(bf16[768,128]{1,0:T(8,128)(2,1)S(1)} %get-tuple-element.228, bf16[8,16,128,128]{3,2,1,0:T(8,128)(2,1)} %get-tuple-element.226, s32[]{:T(128)} %get-tuple-element.218, f32[768]{0:T(1024)S(1)} %get-tuple-element.227, f32[16,128]{1,0:T(8,128)S(1)} %fusion.86), kind=kOutput, calls=%fused_computation.6.clone.1 | convolution fusion | flops 416806912 | bytes 3886592 | tf_op jit(solution)/shard_map/while/body/eval_jaxpr/sbw,mw->sbm/dot_general | solution.py:85
  248.0 3.0 broadcast.163.clone
  251.0 89.1 %while.22 = (s32[]{:T(128)}, bf16[8,16,128,128]{3,2,1,0:T(8,128)(2,1)}, bf16[8,16,128,128]{3,2,1,0:T(8,128)(2,1)}, f32[768]{0:T(1024)S(1)}, bf16[768,128]{1,0:T(8,128)(2,1)S(1)}, /*index=5*/s32[]{:T(128)}) while((s32[]{:T(128)}, bf16[8,16,128,128]{3,2,1,0:T(8,128)(2,1)}, bf16[8,16,128,128]{3,2,1,0:T(8,128)(2,1)}, f32[768]{0:T(1024)S(1)}, ...), condition=%wide.region_14.15_spmd, body=%wide.region_10.14_spmd.sunk | while | flops 958394368 | bytes 13063241 | solution.py:165
  252.4 3.5 %convert_reduce_fusion.14 = (f32[16,128]{1,0:T(8,128)S(1)}, bf16[16,128,768]{2,1,0:T(8,128)(2,1)S(1)}) fusion(bf16[768,128]{1,0:T(8,128)(2,1)S(1)} %get-tuple-element.210, bf16[8,16,128,128]{3,2,1,0:T(8,128)(2,1)} %get-tuple-element.208, s32[]{:T(128)} %get-tuple-element.200, f32[768]{0:T(1024)S(1)} %get-tuple-element.209, f32[16,128]{1,0:T(8,128)S(1)} %fusion.93), kind=kOutput, calls=%fused_computation.42.clone.1 | convolution fusion | flops 416806912 | bytes 3886592 | tf_op jit(solution)/shard_map/while/body/eval_jaxpr/sbw,mw->sbm/dot_general | solution.py:85
  263.5 3.5 %convert_reduce_fusion.14 = (f32[16,128]{1,0:T(8,128)S(1)}, bf16[16,128,768]{2,1,0:T(8,128)(2,1)S(1)}) fusion(bf16[768,128]{1,0:T(8,128)(2,1)S(1)} %get-tuple-element.210, bf16[8,16,128,128]{3,2,1,0:T(8,128)(2,1)} %get-tuple-element.208, s32[]{:T(128)} %get-tuple-element.200, f32[768]{0:T(1024)S(1)} %get-tuple-element.209, f32[16,128]{1,0:T(8,128)S(1)} %fusion.93), kind=kOutput, calls=%fused_computation.42.clone.1 | convolution fusion | flops 416806912 | bytes 3886592 | tf_op jit(solution)/shard_map/while/body/eval_jaxpr/sbw,mw->sbm/dot_general | solution.py:85
  274.7 3.5 %convert_reduce_fusion.14 = (f32[16,128]{1,0:T(8,128)S(1)}, bf16[16,128,768]{2,1,0:T(8,128)(2,1)S(1)}) fusion(bf16[768,128]{1,0:T(8,128)(2,1)S(1)} %get-tuple-element.210, bf16[8,16,128,128]{3,2,1,0:T(8,128)(2,1)} %get-tuple-element.208, s32[]{:T(128)} %get-tuple-element.200, f32[768]{0:T(1024)S(1)} %get-tuple-element.209, f32[16,128]{1,0:T(8,128)S(1)} %fusion.93), kind=kOutput, calls=%fused_computation.42.clone.1 | convolution fusion | flops 416806912 | bytes 3886592 | tf_op jit(solution)/shard_map/while/body/eval_jaxpr/sbw,mw->sbm/dot_general | solution.py:85
  285.8 3.5 %convert_reduce_fusion.14 = (f32[16,128]{1,0:T(8,128)S(1)}, bf16[16,128,768]{2,1,0:T(8,128)(2,1)S(1)}) fusion(bf16[768,128]{1,0:T(8,128)(2,1)S(1)} %get-tuple-element.210, bf16[8,16,128,128]{3,2,1,0:T(8,128)(2,1)} %get-tuple-element.208, s32[]{:T(128)} %get-tuple-element.200, f32[768]{0:T(1024)S(1)} %get-tuple-element.209, f32[16,128]{1,0:T(8,128)S(1)} %fusion.93), kind=kOutput, calls=%fused_computation.42.clone.1 | convolution fusion | flops 416806912 | bytes 3886592 | tf_op jit(solution)/shard_map/while/body/eval_jaxpr/sbw,mw->sbm/dot_general | solution.py:85
  297.0 3.5 %convert_reduce_fusion.14 = (f32[16,128]{1,0:T(8,128)S(1)}, bf16[16,128,768]{2,1,0:T(8,128)(2,1)S(1)}) fusion(bf16[768,128]{1,0:T(8,128)(2,1)S(1)} %get-tuple-element.210, bf16[8,16,128,128]{3,2,1,0:T(8,128)(2,1)} %get-tuple-element.208, s32[]{:T(128)} %get-tuple-element.200, f32[768]{0:T(1024)S(1)} %get-tuple-element.209, f32[16,128]{1,0:T(8,128)S(1)} %fusion.93), kind=kOutput, calls=%fused_computation.42.clone.1 | convolution fusion | flops 416806912 | bytes 3886592 | tf_op jit(solution)/shard_map/while/body/eval_jaxpr/sbw,mw->sbm/dot_general | solution.py:85
  308.1 3.5 %convert_reduce_fusion.14 = (f32[16,128]{1,0:T(8,128)S(1)}, bf16[16,128,768]{2,1,0:T(8,128)(2,1)S(1)}) fusion(bf16[768,128]{1,0:T(8,128)(2,1)S(1)} %get-tuple-element.210, bf16[8,16,128,128]{3,2,1,0:T(8,128)(2,1)} %get-tuple-element.208, s32[]{:T(128)} %get-tuple-element.200, f32[768]{0:T(1024)S(1)} %get-tuple-element.209, f32[16,128]{1,0:T(8,128)S(1)} %fusion.93), kind=kOutput, calls=%fused_computation.42.clone.1 | convolution fusion | flops 416806912 | bytes 3886592 | tf_op jit(solution)/shard_map/while/body/eval_jaxpr/sbw,mw->sbm/dot_general | solution.py:85
  319.3 3.5 %convert_reduce_fusion.14 = (f32[16,128]{1,0:T(8,128)S(1)}, bf16[16,128,768]{2,1,0:T(8,128)(2,1)S(1)}) fusion(bf16[768,128]{1,0:T(8,128)(2,1)S(1)} %get-tuple-element.210, bf16[8,16,128,128]{3,2,1,0:T(8,128)(2,1)} %get-tuple-element.208, s32[]{:T(128)} %get-tuple-element.200, f32[768]{0:T(1024)S(1)} %get-tuple-element.209, f32[16,128]{1,0:T(8,128)S(1)} %fusion.93), kind=kOutput, calls=%fused_computation.42.clone.1 | convolution fusion | flops 416806912 | bytes 3886592 | tf_op jit(solution)/shard_map/while/body/eval_jaxpr/sbw,mw->sbm/dot_general | solution.py:85
  330.4 3.5 %convert_reduce_fusion.14 = (f32[16,128]{1,0:T(8,128)S(1)}, bf16[16,128,768]{2,1,0:T(8,128)(2,1)S(1)}) fusion(bf16[768,128]{1,0:T(8,128)(2,1)S(1)} %get-tuple-element.210, bf16[8,16,128,128]{3,2,1,0:T(8,128)(2,1)} %get-tuple-element.208, s32[]{:T(128)} %get-tuple-element.200, f32[768]{0:T(1024)S(1)} %get-tuple-element.209, f32[16,128]{1,0:T(8,128)S(1)} %fusion.93), kind=kOutput, calls=%fused_computation.42.clone.1 | convolution fusion | flops 416806912 | bytes 3886592 | tf_op jit(solution)/shard_map/while/body/eval_jaxpr/sbw,mw->sbm/dot_general | solution.py:85
  340.1 7.3 %maximum_select_fusion = bf16[1,128,2,128,128]{4,3,2,1,0:T(8,128)(2,1)} fusion(bf16[1,128,1,128,128]{4,3,2,1,0:T(8,128)(2,1)} %bitcast.28, bf16[1,128,1,128,128]{4,3,2,1,0:T(8,128)(2,1)} %bitcast.26, pred[128,2]{1,0:T(8,128)(4,1)S(1)} %iota_compare_fusion.2), kind=kLoop, calls=%fused_computation.73 | loop fusion | flops 8388608 | bytes 16777472 | tf_op jit(solution)/shard_map/jit(_where)/select_n | solution.py:169
  (138 shorter events, 138.2 us)
Async XLA Ops:
  22.1 16.1 %copy-start.1 = (s32[1,1,1,3,1024]{4,2,3,1,0:T(1,128)S(1)}, s32[1,1,1,3,1024]{4,2,3,1,0:T(1,128)}, u32[]{:S(2)}) copy-start(s32[1,1,1,3,1024]{4,2,3,1,0:T(1,128)} %param.12) | copy-start | bytes 36868
  22.1 111.3 %copy-start = (s32[16384,1]{0,1:T(1,128)S(1)}, s32[16384,1]{0,1:T(1,128)}, u32[]{:S(2)}) copy-start(s32[16384,1]{0,1:T(1,128)} %param.10) | copy-start | bytes 196612
  22.1 111.5 %copy-start.2 = (f32[7]{0:T(128)S(1)}, f32[7]{0:T(128)}, u32[]{:S(2)}) copy-start(f32[7]{0:T(128)} %constant.134.clone) | copy-start | bytes 88
  22.1 124.3 %all-to-all-start = ((bf16[128,1,128,128]{3,2,1,0:T(8,128)(2,1)}), bf16[128,1,128,128]{3,2,1,0:T(8,128)(2,1)}, u32[]{:S(2)}, u32[]{:S(2)}) async-start(bf16[128,1,128,128]{3,2,1,0:T(8,128)(2,1)} %get-tuple-element.111), calls=%async_computation | async-start | bytes 8388608 | tf_op jit(solution)/shard_map/all_to_all | solution.py:52
  35.5 98.7 %collective-permute-start = (bf16[1,1,1,1,128,128]{5,4,3,2,1,0:T(8,128)(2,1)S(1)}, bf16[1,1,1,1,128,128]{5,4,3,2,1,0:T(8,128)(2,1)S(1)}, u32[]{:S(2)}, u32[]{:S(2)}) collective-permute-start(bf16[1,1,1,1,128,128]{5,4,3,2,1,0:T(8,128)(2,1)S(1)} %fusion.58), channel_id=1, source_target_pairs={{0,32},{32,64},{64,96},{96,0},{1,33},{33,65},{65,97},{97,1},{2,34}... | collective-permute-start | bytes 98312 | tf_op jit(solution)/shard_map/ppermute | solution.py:30
  36.8 97.3 %collective-permute-start.1 = (bf16[1,1,1,1,128,128]{5,4,3,2,1,0:T(8,128)(2,1)S(1)}, bf16[1,1,1,1,128,128]{5,4,3,2,1,0:T(8,128)(2,1)S(1)}, u32[]{:S(2)}, u32[]{:S(2)}) collective-permute-start(bf16[1,1,1,1,128,128]{5,4,3,2,1,0:T(8,128)(2,1)S(1)} %fusion.58), channel_id=1, source_target_pairs={{32,0},{64,32},{96,64},{0,96},{33,1},{65,33},{97,65},{1,97},{34,2}... | collective-permute-start | bytes 98312 | tf_op jit(solution)/shard_map/ppermute | solution.py:32
  134.2 5.5 %collective-permute-start.2 = (bf16[3,1,1,1,128,128]{5,4,3,2,1,0:T(8,128)(2,1)S(1)}, bf16[3,1,1,1,128,128]{5,4,3,2,1,0:T(8,128)(2,1)S(1)}, u32[]{:S(2)}, u32[]{:S(2)}) collective-permute-start(bf16[3,1,1,1,128,128]{5,4,3,2,1,0:T(8,128)(2,1)S(1)} %pad_maximum_fusion.1), channel_id=1, source_target_pairs={{0,8},{8,16},{16,24},{24,0},{1,9},{9,17},{17,25},{25,1},{2,10},{10... | collective-permute-start | bytes 294920 | tf_op jit(solution)/shard_map/ppermute | solution.py:30
  134.3 5.4 %collective-permute-start.3 = (bf16[3,1,1,1,128,128]{5,4,3,2,1,0:T(8,128)(2,1)S(1)}, bf16[3,1,1,1,128,128]{5,4,3,2,1,0:T(8,128)(2,1)S(1)}, u32[]{:S(2)}, u32[]{:S(2)}) collective-permute-start(bf16[3,1,1,1,128,128]{5,4,3,2,1,0:T(8,128)(2,1)S(1)} %pad_maximum_fusion.1), channel_id=1, source_target_pairs={{8,0},{16,8},{24,16},{0,24},{9,1},{17,9},{25,17},{1,25},{10,2},{18... | collective-permute-start | bytes 294920 | tf_op jit(solution)/shard_map/ppermute | solution.py:32
  139.7 3.7 %collective-permute-start.4 = (bf16[3,3,1,1,128,128]{5,4,3,2,1,0:T(8,128)(2,1)S(1)}, bf16[3,3,1,1,128,128]{5,4,3,2,1,0:T(8,128)(2,1)S(1)}, u32[]{:S(2)}, u32[]{:S(2)}) collective-permute-start(bf16[3,3,1,1,128,128]{5,4,3,2,1,0:T(8,128)(2,1)S(1)} %pad_maximum_fusion), channel_id=1, source_target_pairs={{0,1},{1,2},{2,3},{3,4},{4,5},{5,6},{6,7},{7,0},{8,9},{9,10},{10,1... | collective-permute-start | bytes 884744 | tf_op jit(solution)/shard_map/ppermute | solution.py:30
  139.7 6.5 %collective-permute-start.5 = (bf16[3,3,1,1,128,128]{5,4,3,2,1,0:T(8,128)(2,1)S(1)}, bf16[3,3,1,1,128,128]{5,4,3,2,1,0:T(8,128)(2,1)S(1)}, u32[]{:S(2)}, u32[]{:S(2)}) collective-permute-start(bf16[3,3,1,1,128,128]{5,4,3,2,1,0:T(8,128)(2,1)S(1)} %pad_maximum_fusion), channel_id=1, source_target_pairs={{1,0},{2,1},{3,2},{4,3},{5,4},{6,5},{7,6},{0,7},{9,8},{10,9},{11,1... | collective-permute-start | bytes 884744 | tf_op jit(solution)/shard_map/ppermute | solution.py:32
  146.4 101.7 %all-to-all-start.1 = ((bf16[128,1,128,128]{3,2,1,0:T(8,128)(2,1)}), bf16[128,1,128,128]{3,2,1,0:T(8,128)(2,1)}, u32[]{:S(2)}, u32[]{:S(2)}) async-start(bf16[128,1,128,128]{3,2,1,0:T(8,128)(2,1)} %get-tuple-element.112), calls=%async_computation.1 | async-start | bytes 8388608 | tf_op jit(solution)/shard_map/all_to_all | solution.py:52
where the time goes:
time: 351 us; the launch traced here: 347 us
  matrix products  156 us (44%)
  blocking collectives  91.6 us (26%)
  other arithmetic  39.9 us (11%)
  starting transfers between devices  27.9 us (8%)
  local copies, waits for them, and re-layouts  22.3 us (6%)
  waiting for transfers between devices  8.09 us (2%)
    psum x4, blocking collectives, over_axes(): return functools.reduce(lax.psum, axes, shard)  91.6 us
    dot_general x16, matrix products, pair_forces(): jnp.einsum('sbw,mw->sbm', slot_rows, ghost_set, preferred_element_type=jn...  55.7 us
    dot_general x16, matrix products, pair_forces(): jnp.einsum('sbm,mw->sbw', ghost_kernel, ghost_set, preferred_element_type...  46.2 us
    dot_general x16, matrix products, pair_forces(): jnp.einsum('sbw,scw->sbc', slot_rows, slot_rows, preferred_element_type=j...  32.1 us
    reduce_sum x16, other arithmetic, pair_forces(): own_sq = jnp.sum(rows_f * rows_f, axis=-1)  22.1 us
    dot_general x16, matrix products, pair_forces(): jnp.einsum('sbc,scw->sbw', own_kernel, slot_rows, preferred_element_type=...  21.6 us
    all_to_all x2, starting transfers between devices, exchange_in_groups(): lax.all_to_all(group, axis, split_axis=split_dim, concat_axis=concat_dim,...  21.5 us
    gather x1, local copies, waits for them, and re-layouts, per_device(): jnp.take(seg_rows, source_block, axis=0)  10.8 us
  transfers between devices with their start and end apart: 8, of which 3 were waited for; matrix products, arithmetic and copies ran while one was open for 28% of the time, Pallas kernels for 0%

commit v1 on v0

v1 whole, which is shorter than its diff:
```python
import functools
import math

import jax
import jax.numpy as jnp
from jax import lax
from jax.experimental import pallas as pl
from jax.experimental.pallas import tpu as pltpu
from jax.sharding import PartitionSpec as P

AXES = ("gx", "gy", "gz")

sharpness = 8.0
force_gain = 2.0
radius_eps = 0.001
LOG2E = 1.0 / math.log(2.0)
LN2 = math.log(2.0)
EXTRA = 8
DIGIT = 64
GROUP = 8


def bisect_cuts(histogram):
    running = jnp.cumsum(histogram, axis=1, dtype=jnp.int32)
    total_cost = running[:, -1]
    below = (2 * running < total_cost[:, None]).astype(jnp.int32)
    position = jnp.sum(below, axis=1, dtype=jnp.int32)
    before = jnp.sum(histogram * below, axis=1, dtype=jnp.int32)
    bins_index = lax.broadcasted_iota(jnp.int32, histogram.shape, 1)
    at_cut = jnp.sum(
        jnp.where(bins_index == position[:, None], histogram, 0), axis=1, dtype=jnp.int32
    )
    remain = (total_cost - 2 * before).astype(jnp.float32)
    return (
        position.astype(jnp.float32) + remain / (2 * at_cut).astype(jnp.float32)
    ) / histogram.shape[1]


def pack_body(owners, seg, tails, first, second, seen, sem, tail_sem):
    blocks, rows, _ = seg.shape
    devices = first.shape[0]
    tail_copy = pltpu.make_async_copy(tails, first.at[:, pl.ds(rows, EXTRA), :], tail_sem)
    tail_copy.start()

    def clear(i, carry):
        seen[i] = 0
        return carry

    lax.fori_loop(0, devices, clear, 0, unroll=8)

    def place(j, carry):
        owner = owners[j]
        rank = seen[owner]
        seen[owner] = rank + 1

        @pl.when(rank == 0)
        def _():
            pltpu.make_async_copy(seg.at[j], first.at[owner, pl.ds(0, rows), :], sem).start()

        @pl.when(rank == 1)
        def _():
            pltpu.make_async_copy(seg.at[j], second.at[owner, pl.ds(0, rows), :], sem).start()

        return carry

    lax.fori_loop(0, blocks, place, 0, unroll=4)
    pltpu.make_async_copy(seg, first.at[:, pl.ds(0, rows), :], sem).wait()
    tail_copy.wait()


def pack(own_owners, seg_rows, tails, devices):
    blocks, rows, width = seg_rows.shape
    out = jax.ShapeDtypeStruct((devices, rows + EXTRA, width), seg_rows.dtype)
    return pl.pallas_call(
        pack_body,
        grid_spec=pltpu.PrefetchScalarGridSpec(
            num_scalar_prefetch=1,
            grid=(1,),
            in_specs=[
                pl.BlockSpec(memory_space=pl.ANY),
                pl.BlockSpec(memory_space=pl.ANY),
            ],
            out_specs=[pl.BlockSpec(out.shape, lambda i, o: (0, 0, 0))] * 2,
            scratch_shapes=[
                pltpu.SMEM((devices,), jnp.int32),
                pltpu.SemaphoreType.DMA,
                pltpu.SemaphoreType.DMA,
            ],
        ),
        out_shape=[out, out],
        compiler_params=pltpu.CompilerParams(vmem_limit_bytes=40 << 20),
        name="pack",
    )(own_owners, seg_rows, tails)


def fill_body(tails, send, out, sem):
    rows = out.shape[1] - EXTRA
    copy = pltpu.make_async_copy(tails, out.at[:, pl.ds(rows, EXTRA), :], sem)
    copy.start()
    copy.wait()


def fill_tails(tails, send):
    return pl.pallas_call(
        fill_body,
        in_specs=[pl.BlockSpec(memory_space=pltpu.VMEM), pl.BlockSpec(memory_space=pl.ANY)],
        out_specs=pl.BlockSpec(memory_space=pl.ANY),
        out_shape=jax.ShapeDtypeStruct(send.shape, send.dtype),
        scratch_shapes=[pltpu.SemaphoreType.DMA],
        input_output_aliases={1: 0},
        name="fill",
    )(tails, send)


def slot_forces(x, ghost_t, ghost_aug, ghost_sq, eye):
    rows = x.shape[0]
    x16 = x * jnp.asarray(2.0 * sharpness, x.dtype)
    own = lax.dot_general(x, x16, (((1,), (1,)), ((), ())), preferred_element_type=jnp.float32)
    diag = jnp.where(eye, own, 0.0)
    scale = LN2 / (2.0 * sharpness)
    sq_row = jnp.sum(diag, axis=0, keepdims=True) * scale
    sq_col = jnp.sum(diag, axis=1, keepdims=True) * scale + LN2 * radius_eps
    shift = sharpness * radius_eps
    top = sharpness * LOG2E

    def weights(inner, right_sq):
        return jnp.exp2((inner + shift) / (sq_col + right_sq) - top).astype(jnp.bfloat16)

    inner = jnp.dot(x, ghost_t, preferred_element_type=jnp.float32)
    own_w = weights(own, sq_row)
    ghost_w = weights(inner, ghost_sq)
    x_aug = jnp.concatenate([x, jnp.ones_like(x)], axis=1)
    total = jnp.dot(ghost_w, ghost_aug, preferred_element_type=jnp.float32)
    total = total + jnp.dot(own_w, x_aug, preferred_element_type=jnp.float32)
    width = x.shape[1]
    pulled, weight_sum = total[:, :width], total[:, width:]
    return force_gain * (pulled - weight_sum * x.astype(jnp.float32))


def force_body(rank, arrivals, recv, ghost_t, ghost_aug, ghost_sq, *rest):
    out = rest[-1]
    rows = out.shape[2]
    step = pl.program_id(0)
    eye = lax.broadcasted_iota(jnp.int32, (rows, rows), 0) == lax.broadcasted_iota(
        jnp.int32, (rows, rows), 1
    )

    def pair(k, carry):
        for m in range(2):
            s = 2 * k + m
            x = recv[s, pl.ds(0, rows), :]
            force = slot_forces(x, ghost_t[...], ghost_aug[...], ghost_sq[...], eye)
            filled = arrivals[step * GROUP + s] > rank
            out[s, 0] = jnp.where(filled, force, 0.0).astype(out.dtype)
        return carry

    lax.fori_loop(0, GROUP // 2, pair, 0)


def pair_forces(rank, arrivals, recv, ghost_t, ghost_aug, ghost_sq, capacity, earlier=None):
    devices, full, width = recv.shape
    rows = full - EXTRA
    pairs = devices * rows * (ghost_t.shape[1] + rows)
    in_specs = [
        pl.BlockSpec((GROUP, full, width), lambda i, a: (i, 0, 0)),
        pl.BlockSpec(ghost_t.shape, lambda i, a: (0, 0)),
        pl.BlockSpec(ghost_aug.shape, lambda i, a: (0, 0)),
        pl.BlockSpec(ghost_sq.shape, lambda i, a: (0, 0)),
    ]
    operands = [arrivals, recv, ghost_t, ghost_aug, ghost_sq]
    aliases = {}
    if earlier is not None:
        in_specs.append(pl.BlockSpec(memory_space=pl.ANY))
        operands.append(earlier)
        aliases = {5: 0}
    return pl.pallas_call(
        functools.partial(force_body, rank),
        grid_spec=pltpu.PrefetchScalarGridSpec(
            num_scalar_prefetch=1,
            grid=(devices // GROUP,),
            in_specs=in_specs,
            out_specs=pl.BlockSpec((GROUP, 1, rows, width), lambda i, a: (i, rank, 0, 0)),
        ),
        out_shape=jax.ShapeDtypeStruct((devices, capacity, rows, width), recv.dtype),
        input_output_aliases=aliases,
        cost_estimate=pl.CostEstimate(
            flops=pairs * width * 6, bytes_accessed=4 * devices * rows * width, transcendentals=2 * pairs
        ),
        compiler_params=pltpu.CompilerParams(vmem_limit_bytes=24 << 20),
        name="forces",
    )(*operands)


def ring(size, step):
    return [(i, (i + step) % size) for i in range(size)]


def per_device(seg_rows, owner_map, ghost_pick, slab_cost):
    count_x = lax.axis_size("gx")
    count_y = lax.axis_size("gy")
    count_z = lax.axis_size("gz")
    devices = count_x * count_y * count_z
    blocks_here, block_rows, width = seg_rows.shape
    capacity = 2
    own_index = lax.axis_index(AXES)
    all_owners = owner_map[:, 0].reshape(devices, blocks_here)
    own_owners = lax.dynamic_index_in_dim(all_owners, own_index, 0, keepdims=False)

    exported = lax.dynamic_index_in_dim(seg_rows, ghost_pick[0, 0], 0, keepdims=False)
    ghosts = []
    for axis, size in (("gx", count_x), ("gy", count_y), ("gz", count_z)):
        ghosts.append(lax.ppermute(exported, axis, ring(size, 1)))
        ghosts.append(lax.ppermute(exported, axis, ring(size, -1)))

    local_cost = slab_cost[0, 0, 0]
    kinds, bins = local_cost.shape
    share = bins // devices
    costs = local_cost.astype(jnp.float32).reshape(kinds * share, devices).T
    tails = jnp.pad(costs[:, None, :], ((0, 0), (0, EXTRA - 1), (0, width - kinds * share)))
    first, second = pack(own_owners, seg_rows, tails.astype(jnp.bfloat16), devices)

    exchange = functools.partial(
        lax.all_to_all, axis_name=AXES, split_axis=0, concat_axis=0, tiled=True
    )
    first = exchange(first)

    costs = first[:, block_rows, : kinds * share].astype(jnp.float32)
    source = lax.broadcasted_iota(jnp.int32, (7, devices), 1)
    row = lax.broadcasted_iota(jnp.int32, (7, devices), 0)
    half = source // (devices // 2)
    quarter = half * 2 + source // (count_z * count_y // 2) % 2
    member = (row == 0) | (row == 1 + half) | (row == 3 + quarter)
    sums = jnp.dot(
        member.astype(jnp.float32), costs, precision=lax.Precision.HIGHEST
    ).reshape(7, kinds, share)
    mine = jnp.concatenate([sums[:1, 0], sums[1:3, 1], sums[3:, 2]], axis=0)
    high = jnp.floor(mine * (1.0 / DIGIT))
    low = mine - DIGIT * high
    tile = jnp.pad(
        jnp.concatenate([high, low], axis=1), ((0, EXTRA - 7), (0, width - 2 * share))
    ).astype(jnp.bfloat16)
    tails = jnp.broadcast_to(tile[None], (devices, EXTRA, width))
    second = exchange(fill_tails(tails, second))

    ghost_set = jnp.concatenate(ghosts, axis=0)
    ghost_float = ghost_set.astype(jnp.float32)
    ghost_sq = jnp.sum(ghost_float * ghost_float, axis=-1)[None] * LN2
    ghost_t = (ghost_set * jnp.asarray(2.0 * sharpness, jnp.bfloat16)).T
    ghost_aug = jnp.concatenate([ghost_set, jnp.ones_like(ghost_set)], axis=1)
    arrivals = jnp.sum((all_owners == own_index).astype(jnp.int32), axis=1, dtype=jnp.int32)

    forces = pair_forces(0, arrivals, first, ghost_t, ghost_aug, ghost_sq, capacity)
    forces = pair_forces(1, arrivals, second, ghost_t, ghost_aug, ghost_sq, capacity, forces)

    digits = second[:, block_rows : block_rows + 7, : 2 * share].astype(jnp.float32)
    whole = DIGIT * digits[:, :, :share] + digits[:, :, share:]
    histogram = whole.transpose(1, 2, 0).reshape(7, bins).astype(jnp.int32)
    extent = jnp.array([count_x, count_y, count_y, count_z, count_z, count_z, count_z], jnp.float32)
    cut_points = bisect_cuts(histogram) * extent
    return (forces[None], cut_points)


def solution(mesh):
    in_specs = (P(AXES, None, None), P(), P(AXES, None), P("gx", "gy", "gz", None, None))
    out_specs = (P(AXES, None, None, None, None), P())
    return jax.shard_map(
        per_device, mesh=mesh, in_specs=in_specs, out_specs=out_specs, check_vma=False
    )
```

time: 351 us -> 249 us (0.71)
  matrix products: 156 us -> 0.19 us
  Pallas kernels: 0 us -> 103 us
  waiting for transfers between devices: 8.09 us -> 99.8 us
  blocking collectives: 91.6 us -> 0 us
  other arithmetic: 39.9 us -> 5.86 us
  local copies, waits for them, and re-layouts: 22.3 us -> 11.2 us
    dot_general x64 -> x1, matrix products: 156 us -> 0.19 us  [per_device(): jnp.dot(member.astype(jnp.float32), costs, precision=lax.Precision.HIGHEST)]
    pallas_call x0 -> x4, Pallas kernels: none -> 103 us  [the longest x2 92.9 us: pair_forces(): pl.pallas_call(functools.partial(force_body, rank), grid_spec=pltpu.Prefe...]
    psum x4 -> x0, blocking collectives: 91.6 us -> none  [over_axes(): return functools.reduce(lax.psum, axes, shard)]
    all_to_all x2, waiting for transfers between devices: 0.01 us -> 55.5 us  [the longest x1 55.5 us: per_device(): first = exchange(first)]
    ppermute x6, waiting for transfers between devices: 8.09 us -> 44.3 us  [the longest x3 41.1 us: per_device(): ghosts.append(lax.ppermute(exported, axis, ring(size, 1)))]
    reduce_sum x20 -> x2, other arithmetic: 22.7 us -> 0.51 us  [the longest x1 0.34 us: bisect_cuts(): position = jnp.sum(below, axis=1, dtype=jnp.int32)]
    select_n x6 -> x0, other arithmetic: 12.8 us -> none  [the longest x1 7.28 us: per_device(): jnp.where(valid_slot[:, :, None, None], forces, jnp.zeros((), jnp.bfloat16))]
    gather x1 -> x0, local copies, waits for them, and re-layouts: 10.8 us -> none  [per_device(): jnp.take(seg_rows, source_block, axis=0)]
  transfers between devices with their start and end apart: 8 -> 8, of which waited for: 3 -> 3; matrix products, arithmetic and copies ran while one was open for 28% -> 1% of each run, Pallas kernels for 0% -> 19%
where the time goes in v1:
time: 249 us; the launch traced here: 248 us
  Pallas kernels  103 us (41%)
  waiting for transfers between devices  99.8 us (40%)
  starting transfers between devices  26.8 us (11%)
  local copies, waits for them, and re-layouts  11.2 us (4%)
  other arithmetic  5.86 us (2%)
    pallas_call x2, Pallas kernels, pair_forces(): pl.pallas_call(functools.partial(force_body, rank), grid_spec=pltpu.Prefe...  92.9 us
    all_to_all x1, waiting for transfers between devices, per_device(): first = exchange(first)  55.5 us
    ppermute x3, waiting for transfers between devices, per_device(): ghosts.append(lax.ppermute(exported, axis, ring(size, 1)))  41.1 us
    all_to_all x1, starting transfers between devices, per_device(): first = exchange(first)  11.9 us
    pallas_call x1, Pallas kernels, pack(): pl.pallas_call(pack_body, grid_spec=pltpu.PrefetchScalarGridSpec(num_scal...  8.35 us
    unnamed x16, local copies, waits for them, and re-layouts  6.46 us
    all_to_all x1, starting transfers between devices, per_device(): second = exchange(fill_tails(tails, second))  6.01 us
    ppermute x3, starting transfers between devices, per_device(): ghosts.append(lax.ppermute(exported, axis, ring(size, 1)))  5.58 us
  transfers between devices with their start and end apart: 8, of which 3 were waited for; matrix products, arithmetic and copies ran while one was open for 1% of the time, Pallas kernels for 19%

profile of v1, /device:TPU:1, one launch (start us, length us, event | category | flops | bytes accessed | tf_op | source)
XLA Modules:
  0.0 248.4 jit_solution(9157896620357918905)
XLA Ops:
  0.6 0.7 convert_reduce_fusion.2
  1.5 0.7 dynamic-slice_bitcast_fusion.1.owners
  2.3 2.2 copy-done.2
  4.5 8.3 %pack.1 = (bf16[128,136,128]{2,1,0:T(8,128)(2,1)S(1)}, bf16[128,136,128]{2,1,0:T(8,128)(2,1)S(1)}) custom-call(s32[128]{0:T(128)S(1)} %dynamic-slice_bitcast_fusion.1.owners, bf16[128,128,128]{2,1,0:T(8,128)(2,1)S(1)} %copy-done.2, bf16[128,8,128]{2,1,0:T(8,128)(2,1)S(1)} %pad.11.tails), custom_call_target="tpu_custom_call" | custom-call | tf_op jit(solution)/shard_map/pack/pallas_call | solution.py:74
  12.9 2.1 copy-done
  15.0 2.1 copy-done.1
  17.1 11.9 %all-to-all-start = ((bf16[128,136,128]{2,1,0:T(8,128)(2,1)}), bf16[128,136,128]{2,1,0:T(8,128)(2,1)}, u32[]{:S(2)}, u32[]{:S(2)}) async-start(bf16[128,136,128]{2,1,0:T(8,128)(2,1)} %copy-done.1), calls=%async_computation | async-start | bytes 8912896 | tf_op jit(solution)/shard_map/all_to_all | solution.py:225
  29.0 55.5 %all-to-all-done.recv = bf16[128,136,128]{2,1,0:T(8,128)(2,1)} async-done(((bf16[128,136,128]{2,1,0:T(8,128)(2,1)}), bf16[128,136,128]{2,1,0:T(8,128)(2,1)}, u32[]{:S(2)}, u32[]{:S(2)}) %all-to-all-start) | async-done | bytes 4456480 | tf_op jit(solution)/shard_map/all_to_all | solution.py:225
  84.5 1.0 slice.40
  85.6 0.2 fusion.2
  85.9 0.7 broadcast_in_dim.10.tails
  86.7 1.7 fill.1
  88.4 6.0 %all-to-all-start.1 = ((bf16[128,136,128]{2,1,0:T(8,128)(2,1)}), bf16[128,136,128]{2,1,0:T(8,128)(2,1)}, u32[]{:S(2)}, u32[]{:S(2)}) async-start(bf16[128,136,128]{2,1,0:T(8,128)(2,1)} %fill.1), calls=%async_computation.1 | async-start | bytes 8912896 | tf_op jit(solution)/shard_map/all_to_all | solution.py:243
  95.0 0.8 dynamic-slice_bitcast_fusion
  95.8 1.4 collective-permute-start
  97.2 1.3 collective-permute-start.1
  98.5 1.4 collective-permute-start.2
  99.8 1.3 collective-permute-start.3
  101.2 2.9 %collective-permute-start.4 = (bf16[128,128]{1,0:T(8,128)(2,1)S(1)}, bf16[128,128]{1,0:T(8,128)(2,1)S(1)}, u32[]{:S(2)}, u32[]{:S(2)}) collective-permute-start(bf16[128,128]{1,0:T(8,128)(2,1)S(1)} %dynamic-slice_bitcast_fusion), channel_id=1, source_target_pairs={{0,1},{1,2},{2,3},{3,4},{4,5},{5,6},{6,7},{7,0},{8,9},{9,10},{10,1... | collective-permute-start | bytes 98312 | tf_op jit(solution)/shard_map/ppermute | solution.py:212
  104.2 41.1 %collective-permute-done = bf16[128,128]{1,0:T(8,128)(2,1)S(1)} collective-permute-done((bf16[128,128]{1,0:T(8,128)(2,1)S(1)}, bf16[128,128]{1,0:T(8,128)(2,1)S(1)}, u32[]{:S(2)}, u32[]{:S(2)}) %collective-permute-start) | collective-permute-done | bytes 32800 | tf_op jit(solution)/shard_map/ppermute | solution.py:212
  145.3 0.7 collective-permute-start.5
  146.1 3.1 %collective-permute-done.5 = bf16[128,128]{1,0:T(8,128)(2,1)S(1)} collective-permute-done((bf16[128,128]{1,0:T(8,128)(2,1)S(1)}, bf16[128,128]{1,0:T(8,128)(2,1)S(1)}, u32[]{:S(2)}, u32[]{:S(2)}) %collective-permute-start.5) | collective-permute-done | bytes 32800 | tf_op jit(solution)/shard_map/ppermute | solution.py:213
  149.7 46.4 %forces.2.rest_0_ = bf16[128,2,128,128]{3,2,1,0:T(8,128)(2,1)} custom-call(s32[128]{0:T(128)S(1)} %convert_reduce_fusion.1.arrivals, bf16[128,136,128]{2,1,0:T(8,128)(2,1)} %all-to-all-done.recv, bf16[128,768]{1,0:T(8,128)(2,1)S(1)} %copy.24.ghost_t, bf16[768,256]{1,0:T(8,128)(2,1)S(1)} %concatenate.16.ghost_aug, f32[1,768]{1,0:T(1,128)S(1)} %mul.80.ghost_sq), custom_call_target="tpu_custom_call" | custom-call | flops 11274289152 | bytes 8388608 | tf_op jit(solution)/shard_map/forces/pallas_call | solution.py:176
  196.1 1.0 slice_convert_fusion
  197.1 0.2 fusion.1
  197.5 2.0 reduce-window.6
  199.5 0.2 copy.26
  199.7 0.3 slice_reduce_fusion
  200.6 0.3 convert_reduce_fusion
  200.9 0.4 select_reduce_fusion.1
  201.4 0.5 multiply_multiply_fusion
  201.9 46.5 %forces.3 = bf16[128,2,128,128]{3,2,1,0:T(8,128)(2,1)} custom-call(s32[128]{0:T(128)S(1)} %convert_reduce_fusion.1.arrivals, bf16[128,136,128]{2,1,0:T(8,128)(2,1)} %all-to-all-done.1.recv, bf16[128,768]{1,0:T(8,128)(2,1)S(1)} %copy.24.ghost_t, bf16[768,256]{1,0:T(8,128)(2,1)S(1)} %concatenate.16.ghost_aug, ...), custom_call_target="tpu_custom_call", output_to_operand_aliasing={{}: (5, {})} | custom-call | flops 11274289152 | bytes 8388608 | tf_op jit(solution)/shard_map/forces/pallas_call | solution.py:176
  (45 shorter events, 1.8 us)
Async XLA Ops:
  2.3 2.2 copy-start.2
  12.9 2.1 copy-start
  15.0 2.1 copy-start.1
  17.1 67.5 %all-to-all-start = ((bf16[128,136,128]{2,1,0:T(8,128)(2,1)}), bf16[128,136,128]{2,1,0:T(8,128)(2,1)}, u32[]{:S(2)}, u32[]{:S(2)}) async-start(bf16[128,136,128]{2,1,0:T(8,128)(2,1)} %copy-done.1), calls=%async_computation | async-start | bytes 8912896 | tf_op jit(solution)/shard_map/all_to_all | solution.py:225
  88.4 15.7 %copy-start.3 = (s32[16384,1]{0,1:T(1,128)S(1)}, s32[16384,1]{0,1:T(1,128)}, u32[]{:S(2)}) copy-start(s32[16384,1]{0,1:T(1,128)} %param.6) | copy-start | bytes 196612
  88.4 107.7 %all-to-all-start.1 = ((bf16[128,136,128]{2,1,0:T(8,128)(2,1)}), bf16[128,136,128]{2,1,0:T(8,128)(2,1)}, u32[]{:S(2)}, u32[]{:S(2)}) async-start(bf16[128,136,128]{2,1,0:T(8,128)(2,1)} %fill.1), calls=%async_computation.1 | async-start | bytes 8912896 | tf_op jit(solution)/shard_map/all_to_all | solution.py:243
  95.8 49.5 %collective-permute-start = (bf16[128,128]{1,0:T(8,128)(2,1)S(1)}, bf16[128,128]{1,0:T(8,128)(2,1)S(1)}, u32[]{:S(2)}, u32[]{:S(2)}) collective-permute-start(bf16[128,128]{1,0:T(8,128)(2,1)S(1)} %dynamic-slice_bitcast_fusion), channel_id=1, source_target_pairs={{0,32},{32,64},{64,96},{96,0},{1,33},{33,65},{65,97},{97,1},{2,34}... | collective-permute-start | bytes 98312 | tf_op jit(solution)/shard_map/ppermute | solution.py:212
  97.2 48.8 %collective-permute-start.1 = (bf16[128,128]{1,0:T(8,128)(2,1)S(1)}, bf16[128,128]{1,0:T(8,128)(2,1)S(1)}, u32[]{:S(2)}, u32[]{:S(2)}) collective-permute-start(bf16[128,128]{1,0:T(8,128)(2,1)S(1)} %dynamic-slice_bitcast_fusion), channel_id=1, source_target_pairs={{0,96},{32,0},{64,32},{96,64},{1,97},{33,1},{65,33},{97,65},{2,98}... | collective-permute-start | bytes 98312 | tf_op jit(solution)/shard_map/ppermute | solution.py:213
  98.5 47.5 %collective-permute-start.2 = (bf16[128,128]{1,0:T(8,128)(2,1)S(1)}, bf16[128,128]{1,0:T(8,128)(2,1)S(1)}, u32[]{:S(2)}, u32[]{:S(2)}) collective-permute-start(bf16[128,128]{1,0:T(8,128)(2,1)S(1)} %dynamic-slice_bitcast_fusion), channel_id=1, source_target_pairs={{0,8},{8,16},{16,24},{24,0},{1,9},{9,17},{17,25},{25,1},{2,10},{10... | collective-permute-start | bytes 98312 | tf_op jit(solution)/shard_map/ppermute | solution.py:212
  99.8 46.2 %collective-permute-start.3 = (bf16[128,128]{1,0:T(8,128)(2,1)S(1)}, bf16[128,128]{1,0:T(8,128)(2,1)S(1)}, u32[]{:S(2)}, u32[]{:S(2)}) collective-permute-start(bf16[128,128]{1,0:T(8,128)(2,1)S(1)} %dynamic-slice_bitcast_fusion), channel_id=1, source_target_pairs={{0,24},{8,0},{16,8},{24,16},{1,25},{9,1},{17,9},{25,17},{2,26},{10... | collective-permute-start | bytes 98312 | tf_op jit(solution)/shard_map/ppermute | solution.py:213
  101.2 44.9 %collective-permute-start.4 = (bf16[128,128]{1,0:T(8,128)(2,1)S(1)}, bf16[128,128]{1,0:T(8,128)(2,1)S(1)}, u32[]{:S(2)}, u32[]{:S(2)}) collective-permute-start(bf16[128,128]{1,0:T(8,128)(2,1)S(1)} %dynamic-slice_bitcast_fusion), channel_id=1, source_target_pairs={{0,1},{1,2},{2,3},{3,4},{4,5},{5,6},{6,7},{7,0},{8,9},{9,10},{10,1... | collective-permute-start | bytes 98312 | tf_op jit(solution)/shard_map/ppermute | solution.py:212
  145.3 3.9 %collective-permute-start.5 = (bf16[128,128]{1,0:T(8,128)(2,1)S(1)}, bf16[128,128]{1,0:T(8,128)(2,1)S(1)}, u32[]{:S(2)}, u32[]{:S(2)}) collective-permute-start(bf16[128,128]{1,0:T(8,128)(2,1)S(1)} %dynamic-slice_bitcast_fusion), channel_id=1, source_target_pairs={{0,7},{1,0},{2,1},{3,2},{4,3},{5,4},{6,5},{7,6},{8,15},{9,8},{10,9... | collective-permute-start | bytes 98312 | tf_op jit(solution)/shard_map/ppermute | solution.py:213
  196.1 5.3 %copy-start.4 = (f32[7]{0:T(128)S(1)}, f32[7]{0:T(128)}, u32[]{:S(2)}) copy-start(f32[7]{0:T(128)} %constant.105.clone) | copy-start | bytes 88

commit v2 on v1

v2 whole, which is shorter than its diff:
```python
import functools
import math

import jax
import jax.numpy as jnp
import ml_dtypes
import numpy as np
from jax import lax
from jax.experimental import pallas as pl
from jax.experimental.pallas import tpu as pltpu
from jax.sharding import PartitionSpec as P

AXES = ("gx", "gy", "gz")

sharpness = 8.0
force_gain = 2.0
radius_eps = 0.001
LN2 = math.log(2.0)
EXTRA = 8
DIGIT = 64
LOW_AT = 64
LOADS = 8
GROUP = 64
ROWS_OF_CUTS = 7


def bf16_terms(value):
    terms = []
    for _ in range(3):
        terms.append(float(np.float32(value).astype(ml_dtypes.bfloat16)))
        value = value - terms[-1]
    return terms


SHIFT = bf16_terms(sharpness * radius_eps)


def pack_body(owners, seg, tails, first, second, held, seen, load_sem, sem, tail_sem):
    blocks, rows, _ = seg.shape
    devices = first.shape[0]
    part = blocks // LOADS
    loads = [
        pltpu.make_async_copy(
            seg.at[pl.ds(k * part, part)], held.at[pl.ds(k * part, part)], load_sem.at[k]
        )
        for k in range(LOADS)
    ]
    for load in loads:
        load.start()
    tail_copy = pltpu.make_async_copy(tails, first.at[:, pl.ds(rows, EXTRA), :], tail_sem)
    tail_copy.start()

    def clear(i, carry):
        seen[i] = 0
        return carry

    lax.fori_loop(0, devices, clear, 0, unroll=8)

    def place(j, carry):
        owner = owners[j]
        rank = seen[owner]
        seen[owner] = rank + 1

        @pl.when(rank == 0)
        def _():
            pltpu.make_async_copy(held.at[j], first.at[owner, pl.ds(0, rows), :], sem).start()

        @pl.when(rank == 1)
        def _():
            pltpu.make_async_copy(held.at[j], second.at[owner, pl.ds(0, rows), :], sem).start()

        return carry

    for k in range(LOADS):
        loads[k].wait()
        lax.fori_loop(k * part, (k + 1) * part, place, 0, unroll=4)
    pltpu.make_async_copy(held, first.at[:, pl.ds(0, rows), :], sem).wait()
    tail_copy.wait()


def pack(own_owners, seg_rows, tails, devices):
    blocks, rows, width = seg_rows.shape
    out = jax.ShapeDtypeStruct((devices, rows + EXTRA, width), seg_rows.dtype)
    return pl.pallas_call(
        pack_body,
        grid_spec=pltpu.PrefetchScalarGridSpec(
            num_scalar_prefetch=1,
            grid=(1,),
            in_specs=[
                pl.BlockSpec(memory_space=pltpu.HBM),
                pl.BlockSpec(tails.shape, lambda i, o: (0, 0, 0)),
            ],
            out_specs=[pl.BlockSpec(memory_space=pltpu.HBM)] * 2,
            scratch_shapes=[
                pltpu.VMEM((blocks, rows, width), seg_rows.dtype),
                pltpu.SMEM((devices,), jnp.int32),
                pltpu.SemaphoreType.DMA((LOADS,)),
                pltpu.SemaphoreType.DMA,
                pltpu.SemaphoreType.DMA,
            ],
        ),
        out_shape=[out, out],
        cost_estimate=pl.CostEstimate(
            flops=1 << 27, bytes_accessed=4 * blocks * rows * width, transcendentals=0
        ),
        name="pack",
    )(own_owners, seg_rows, tails)


def fold_body(layout, recv, send, out, tails, tile, sem):
    devices, group = layout
    rows = out.shape[1] - EXTRA
    width = out.shape[2]
    load = pltpu.make_async_copy(recv.at[:, pl.ds(rows, EXTRA), :], tails, sem.at[0])
    load.start()
    row = lax.broadcasted_iota(jnp.int32, (EXTRA, devices * EXTRA), 0)
    line = lax.broadcasted_iota(jnp.int32, (EXTRA, devices * EXTRA), 1)
    source = line // EXTRA
    half = source // (devices // 2)
    quarter = half * 2 + source // (group // 2) % 2
    member = ((row == 0) | (row == 1 + half) | (row == 3 + quarter)) & (line % EXTRA == 0)
    member = member.astype(jnp.float32).astype(jnp.bfloat16)
    load.wait()
    costs = tails[...].reshape(devices * EXTRA, width)
    sums = jnp.dot(member, costs, preferred_element_type=jnp.float32)
    high = jnp.floor(sums * (1.0 / DIGIT))
    low = sums - DIGIT * high
    lane = lax.broadcasted_iota(jnp.int32, (EXTRA, width), 1)
    digits = jnp.where(lane < LOW_AT, high, pltpu.roll(low, LOW_AT, 1)).astype(jnp.bfloat16)
    tile[...] = jnp.broadcast_to(digits[None], tile.shape)
    store = pltpu.make_async_copy(tile, out.at[:, pl.ds(rows, EXTRA), :], sem.at[1])
    store.start()
    store.wait()


def fold_tails(recv, send, devices, group):
    width = recv.shape[2]
    return pl.pallas_call(
        functools.partial(fold_body, (devices, group)),
        in_specs=[pl.BlockSpec(memory_space=pltpu.HBM)] * 2,
        out_specs=pl.BlockSpec(memory_space=pltpu.HBM),
        out_shape=jax.ShapeDtypeStruct(send.shape, send.dtype),
        scratch_shapes=[
            pltpu.VMEM((devices, EXTRA, width), send.dtype),
            pltpu.VMEM((devices, EXTRA, width), send.dtype),
            pltpu.SemaphoreType.DMA((2,)),
        ],
        input_output_aliases={1: 0},
        name="fold",
    )(recv, send)


def cuts_body(share, extents, recv, out, tails, sem):
    rows = recv.shape[1] - EXTRA
    devices, _, width = tails.shape
    load = pltpu.make_async_copy(recv.at[:, pl.ds(rows, EXTRA), :], tails, sem)
    load.start()
    load.wait()
    digits = tails[...].astype(jnp.float32)
    digits = digits.reshape(devices * EXTRA, width)
    cost = (DIGIT * digits + pltpu.roll(digits, width - LOW_AT, 1)).reshape(devices, EXTRA, width)
    line = lax.broadcasted_iota(jnp.int32, (EXTRA, width), 0)
    lane = lax.broadcasted_iota(jnp.int32, (EXTRA, width), 1)
    kind = jnp.where(line == 0, 0, jnp.where(line < 3, 1, 2))
    valid = (lane // share == kind) & (line < ROWS_OF_CUTS)
    cost = jnp.where(valid[None], cost, 0.0)
    inside = cost
    step = 1
    while step < devices:
        inside = inside + jnp.concatenate(
            [jnp.zeros((step, EXTRA, width), jnp.float32), inside[:-step]], axis=0
        )
        step *= 2
    whole = inside[devices - 1]
    upto = whole
    step = 1
    while step < share:
        upto = upto + jnp.where(lane % share >= step, pltpu.roll(upto, step, 1), 0.0)
        step *= 2
    total = jnp.sum(whole, axis=1, keepdims=True)
    running = inside + (upto - whole)[None]
    below = (2.0 * running < total[None]) & valid[None]
    below = below.astype(jnp.float32)
    position = jnp.sum(jnp.sum(below, axis=0), axis=1, keepdims=True)
    before = jnp.sum(jnp.sum(below * cost, axis=0), axis=1, keepdims=True)
    place = lax.broadcasted_iota(jnp.int32, (devices, EXTRA, width), 0) + (
        lane % share * devices
    )[None]
    hit = place.astype(jnp.float32) == position[None]
    at_cut = jnp.sum(jnp.sum(jnp.where(hit, cost, 0.0), axis=0), axis=1, keepdims=True)
    cut = (position + (total - 2.0 * before) / (2.0 * at_cut)) * (1.0 / (devices * share))
    extent = jnp.where(line == 0, extents[0], jnp.where(line < 3, extents[1], extents[2]))
    out[...] = cut * extent.astype(jnp.float32)


def cuts(recv, share, extents):
    devices, _, width = recv.shape
    return pl.pallas_call(
        functools.partial(cuts_body, share, extents),
        in_specs=[pl.BlockSpec(memory_space=pltpu.HBM)],
        out_specs=pl.BlockSpec(memory_space=pltpu.VMEM),
        out_shape=jax.ShapeDtypeStruct((EXTRA, width), jnp.float32),
        scratch_shapes=[
            pltpu.VMEM((devices, EXTRA, width), recv.dtype),
            pltpu.SemaphoreType.DMA,
        ],
        name="cuts",
    )(recv)[:ROWS_OF_CUTS, 0]


def force_body(rank, group, arrivals, recv, ghost_t, ghost_aug, ghost_sq, *rest):
    out = rest[-7]
    inners, weight_s, columns = rest[-6:-4], rest[-4:-2], rest[-2:]
    rows = out.shape[2]
    width = out.shape[3]
    ghosts = ghost_t.shape[1]
    batches = group // 2
    step = pl.program_id(0)
    scale = LN2 / (2.0 * sharpness)
    eye = lax.broadcasted_iota(jnp.int32, (rows, rows), 0) == lax.broadcasted_iota(
        jnp.int32, (rows, rows), 1
    )
    lane = lax.broadcasted_iota(jnp.int32, (rows, width), 1)
    ones = (lane < 3).astype(jnp.float32).astype(jnp.bfloat16)

    def batch_of(b):
        return 2 * jnp.clip(b, 0, batches - 1)

    def products(b, inner, column):
        s = batch_of(b)
        x = recv[pl.ds(s, 2), pl.ds(0, rows), :].reshape(2 * rows, width)
        x_aug = jnp.concatenate([x, jnp.concatenate([ones, ones], axis=0)], axis=1)
        inner[:, :ghosts] = jnp.dot(x_aug, ghost_t[...], preferred_element_type=jnp.float32)
        for m in range(2):
            mine = x[m * rows : (m + 1) * rows]
            x16 = mine * jnp.asarray(2.0 * sharpness, mine.dtype)
            inner[m * rows : (m + 1) * rows, ghosts:] = lax.dot_general(
                x_aug[m * rows : (m + 1) * rows],
                jnp.concatenate([x16, shift_lanes()], axis=1),
                (((1,), (1,)), ((), ())),
                preferred_element_type=jnp.float32,
            )
            wide = mine.astype(jnp.float32)
            sq = jnp.sum(wide * wide, axis=1, keepdims=True) * LN2 + 0.5 * LN2 * radius_eps
            column[m * rows : (m + 1) * rows] = jnp.broadcast_to(sq, (rows, width))

    def shift_lanes():
        lanes = jnp.zeros((rows, width), jnp.float32)
        for k, term in enumerate(SHIFT):
            lanes = jnp.where(lane == k, term, lanes)
        return lanes.astype(jnp.bfloat16)

    def two(na, da, nb, db):
        r = 1.0 / (da * db)
        return jnp.exp2(na * (r * db)).astype(jnp.bfloat16), jnp.exp2(nb * (r * da)).astype(jnp.bfloat16)

    def weights(inner, column, weight):
        a, b = slice(0, rows), slice(rows, 2 * rows)
        own = [inner[h, ghosts:] for h in (a, b)]
        den = [
            column[h] + jnp.sum(jnp.where(eye, o, 0.0), axis=0, keepdims=True) * scale
            for h, o in zip((a, b), own)
        ]
        weight[a, ghosts:], weight[b, ghosts:] = two(own[0], den[0], own[1], den[1])
        for t in range(0, ghosts, 2 * width):
            p, q = slice(t, t + width), slice(t + width, t + 2 * width)
            weight[:, p], weight[:, q] = two(
                inner[:, p], column[...] + ghost_sq[:, p], inner[:, q], column[...] + ghost_sq[:, q]
            )

    def settle(b, weight):
        s = batch_of(b)
        total = jnp.dot(weight[:, :ghosts], ghost_aug[...], preferred_element_type=jnp.float32)
        for m in range(2):
            here = slice(m * rows, (m + 1) * rows)
            x = recv[s + m, pl.ds(0, rows), :]
            both = total[here] + jnp.dot(
                weight[here, ghosts:],
                jnp.concatenate([x, jnp.ones_like(x)], axis=1),
                preferred_element_type=jnp.float32,
            )
            force = both[:, :width] - both[:, width:] * x.astype(jnp.float32)
            gain = force_gain * math.exp(-sharpness)
            filled = arrivals[step * group + s + m] > rank
            out[s + m, 0] = jnp.where(filled, gain * force, 0.0).astype(out.dtype)

    def body(m, carry):
        b = 2 * m
        for k in range(2):
            e, o = k % 2, (k + 1) % 2
            products(b + k, inners[e], columns[e])
            weights(inners[o], columns[o], weight_s[o])
            settle(b + k - 2, weight_s[e])
        return carry

    lax.fori_loop(0, (batches + 2 + 2 - 1) // 2, body, 0)


def pair_forces(rank, arrivals, recv, ghost_t, ghost_aug, ghost_sq, capacity, earlier=None):
    devices, full, width = recv.shape
    rows = full - EXTRA
    ghosts = ghost_t.shape[1]
    pairs = devices * rows * (ghosts + rows)
    in_specs = [
        pl.BlockSpec((GROUP, full, width), lambda i, a: (i, 0, 0)),
        pl.BlockSpec(ghost_t.shape, lambda i, a: (0, 0)),
        pl.BlockSpec(ghost_aug.shape, lambda i, a: (0, 0)),
        pl.BlockSpec(ghost_sq.shape, lambda i, a: (0, 0)),
    ]
    operands = [arrivals, recv, ghost_t, ghost_aug, ghost_sq]
    aliases = {}
    if earlier is not None:
        in_specs.append(pl.BlockSpec(memory_space=pl.ANY))
        operands.append(earlier)
        aliases = {5: 0}
    return pl.pallas_call(
        functools.partial(force_body, rank, GROUP),
        grid_spec=pltpu.PrefetchScalarGridSpec(
            num_scalar_prefetch=1,
            grid=(devices // GROUP,),
            in_specs=in_specs,
            out_specs=pl.BlockSpec((GROUP, 1, rows, width), lambda i, a: (i, rank, 0, 0)),
            scratch_shapes=[pltpu.VMEM((2 * rows, ghosts + rows), jnp.float32)] * 2
            + [pltpu.VMEM((2 * rows, ghosts + rows), jnp.bfloat16)] * 2
            + [pltpu.VMEM((2 * rows, width), jnp.float32)] * 2,
        ),
        out_shape=jax.ShapeDtypeStruct((devices, capacity, rows, width), recv.dtype),
        input_output_aliases=aliases,
        cost_estimate=pl.CostEstimate(
            flops=pairs * width * 6, bytes_accessed=4 * devices * rows * width, transcendentals=2 * pairs
        ),
        compiler_params=pltpu.CompilerParams(vmem_limit_bytes=32 << 20),
        name="forces",
    )(*operands)


def ring(size, step):
    return [(i, (i + step) % size) for i in range(size)]


def per_device(seg_rows, owner_map, ghost_pick, slab_cost):
    count_x = lax.axis_size("gx")
    count_y = lax.axis_size("gy")
    count_z = lax.axis_size("gz")
    devices = count_x * count_y * count_z
    blocks_here, block_rows, width = seg_rows.shape
    capacity = 2
    own_index = lax.axis_index(AXES)
    all_owners = owner_map[:, 0].reshape(devices, blocks_here)
    own_owners = lax.dynamic_index_in_dim(all_owners, own_index, 0, keepdims=False)

    exported = lax.dynamic_index_in_dim(seg_rows, ghost_pick[0, 0], 0, keepdims=False)
    ghosts = []
    for axis, size in (("gx", count_x), ("gy", count_y), ("gz", count_z)):
        ghosts.append(lax.ppermute(exported, axis, ring(size, 1)))
        ghosts.append(lax.ppermute(exported, axis, ring(size, -1)))

    local_cost = slab_cost[0, 0, 0]
    kinds, bins = local_cost.shape
    share = bins // devices
    costs = local_cost.astype(jnp.float32).reshape(kinds * share, devices).T
    tails = jnp.pad(costs[:, None, :], ((0, 0), (0, EXTRA - 1), (0, width - kinds * share)))
    first, second = pack(own_owners, seg_rows, tails.astype(jnp.bfloat16), devices)
    first, *ghosts = lax.optimization_barrier((first, *ghosts))

    exchange = functools.partial(
        lax.all_to_all, axis_name=AXES, split_axis=0, concat_axis=0, tiled=True
    )
    first = exchange(first)
    second = exchange(fold_tails(first, second, devices, count_y * count_z))

    ghost_set = jnp.concatenate(ghosts, axis=0)
    ghost_float = ghost_set.astype(jnp.float32)
    ghost_sq = jnp.sum(ghost_float * ghost_float, axis=-1)[None] * LN2 + 0.5 * LN2 * radius_eps
    ghost_t = (ghost_set * jnp.asarray(2.0 * sharpness, jnp.bfloat16)).T
    term = jnp.array(SHIFT + [0.0] * (width - len(SHIFT)), jnp.bfloat16)
    ghost_t = jnp.concatenate(
        [ghost_t, jnp.broadcast_to(term[:, None], (width, ghost_t.shape[1]))], axis=0
    )
    ghost_aug = jnp.concatenate([ghost_set, jnp.ones_like(ghost_set)], axis=1)
    arrivals = jnp.sum((all_owners == own_index).astype(jnp.int32), axis=1, dtype=jnp.int32)

    forces = pair_forces(0, arrivals, first, ghost_t, ghost_aug, ghost_sq, capacity)
    forces = pair_forces(1, arrivals, second, ghost_t, ghost_aug, ghost_sq, capacity, forces)
    cut_points = cuts(second, share, (count_x, count_y, count_z))
    return (forces[None], cut_points)


def solution(mesh):
    in_specs = (P(AXES, None, None), P(), P(AXES, None), P("gx", "gy", "gz", None, None))
    out_specs = (P(AXES, None, None, None, None), P())
    return jax.shard_map(
        per_device, mesh=mesh, in_specs=in_specs, out_specs=out_specs, check_vma=False
    )
```

time: 249 us -> 183 us (0.73)
  waiting for transfers between devices: 99.8 us -> 22.7 us
  blocking collectives: 0 us -> 63.6 us
  Pallas kernels: 103 us -> 71.2 us
  starting transfers between devices: 26.8 us -> 15.4 us
  other arithmetic: 5.86 us -> 1.11 us
  local copies, waits for them, and re-layouts: 11.2 us -> 6.73 us
    all_to_all x0 -> x1, blocking collectives: none -> 63.6 us  [per_device(): first = exchange(first)]
    ppermute x3, waiting for transfers between devices: 41.1 us -> 0.01 us  [per_device(): ghosts.append(lax.ppermute(exported, axis, ring(size, 1)))]
    all_to_all x2 -> x1, waiting for transfers between devices: 55.5 us -> 22.7 us  [per_device(): second = exchange(fold_tails(first, second, devices, count_y * count_z))]
    pallas_call x3 -> x4, Pallas kernels: 94.6 us -> 66 us  [the longest x2 61.6 us: pair_forces(): pl.pallas_call(functools.partial(force_body, rank, GROUP), grid_spec=pltp...]
    all_to_all x2 -> x1, starting transfers between devices: 17.9 us -> 5.91 us  [per_device(): second = exchange(fold_tails(first, second, devices, count_y * count_z))]
    unnamed x16 -> x11, local copies, waits for them, and re-layouts: 6.46 us -> 2.31 us
    ppermute x3, waiting for transfers between devices: 3.15 us -> 0.01 us  [per_device(): ghosts.append(lax.ppermute(exported, axis, ring(size, -1)))]
    pallas_call x1, Pallas kernels: 8.35 us -> 5.21 us  [pack(): pl.pallas_call(pack_body, grid_spec=pltpu.PrefetchScalarGridSpec(num_scal...]
  transfers between devices with their start and end apart: 8 -> 7, of which waited for: 3 -> 1; matrix products, arithmetic and copies ran while one was open for 1% -> 2% of each run, Pallas kernels for 19% -> 19%
where the time goes in v2:
time: 183 us; the launch traced here: 182 us
  Pallas kernels  71.2 us (39%)
  blocking collectives  63.6 us (35%)
  waiting for transfers between devices  22.7 us (12%)
  starting transfers between devices  15.4 us (8%)
  local copies, waits for them, and re-layouts  6.73 us (4%)
    all_to_all x1, blocking collectives, per_device(): first = exchange(first)  63.6 us
    pallas_call x2, Pallas kernels, pair_forces(): pl.pallas_call(functools.partial(force_body, rank, GROUP), grid_spec=pltp...  61.6 us
    all_to_all x1, waiting for transfers between devices, per_device(): second = exchange(fold_tails(first, second, devices, count_y * count_z))  22.7 us
    ppermute x3, starting transfers between devices, per_device(): ghosts.append(lax.ppermute(exported, axis, ring(size, 1)))  6.78 us
    all_to_all x1, starting transfers between devices, per_device(): second = exchange(fold_tails(first, second, devices, count_y * count_z))  5.91 us
    pallas_call x1, Pallas kernels, pack(): pl.pallas_call(pack_body, grid_spec=pltpu.PrefetchScalarGridSpec(num_scal...  5.21 us
  transfers between devices with their start and end apart: 7, of which 1 were waited for; matrix products, arithmetic and copies ran while one was open for 2% of the time, Pallas kernels for 19%

profile of v2, /device:TPU:1, one launch (start us, length us, event | category | flops | bytes accessed | tf_op | source)
XLA Modules:
  0.0 182.2 jit_solution(3395670246927445509)
XLA Ops:
  1.3 0.8 dynamic-slice_bitcast_fusion
  2.0 2.0 %collective-permute-start = (bf16[128,128]{1,0:T(8,128)(2,1)S(1)}, bf16[128,128]{1,0:T(8,128)(2,1)S(1)}, u32[]{:S(2)}, u32[]{:S(2)}) collective-permute-start(bf16[128,128]{1,0:T(8,128)(2,1)S(1)} %dynamic-slice_bitcast_fusion), channel_id=1, source_target_pairs={{0,32},{32,64},{64,96},{96,0},{1,33},{33,65},{65,97},{97,1},{2,34}... | collective-permute-start | bytes 98312 | tf_op jit(solution)/shard_map/ppermute | solution.py:355
  4.1 1.3 collective-permute-start.1
  5.3 1.5 collective-permute-start.2
  6.8 1.4 collective-permute-start.3
  8.3 3.3 %collective-permute-start.4 = (bf16[128,128]{1,0:T(8,128)(2,1)S(1)}, bf16[128,128]{1,0:T(8,128)(2,1)S(1)}, u32[]{:S(2)}, u32[]{:S(2)}) collective-permute-start(bf16[128,128]{1,0:T(8,128)(2,1)S(1)} %dynamic-slice_bitcast_fusion), channel_id=1, source_target_pairs={{0,1},{1,2},{2,3},{3,4},{4,5},{5,6},{6,7},{7,0},{8,9},{9,10},{10,1... | collective-permute-start | bytes 98312 | tf_op jit(solution)/shard_map/ppermute | solution.py:355
  11.5 0.7 convert_reduce_fusion.1
  12.3 0.0 collective-permute-done
  12.3 0.0 collective-permute-start.5
  12.3 1.2 dynamic-slice_bitcast_fusion.1.owners
  13.6 0.1 copy.11
  13.7 0.8 pad.6.tails
  14.5 5.2 %pack.1 = (bf16[128,136,128]{2,1,0:T(8,128)(2,1)}, bf16[128,136,128]{2,1,0:T(8,128)(2,1)}) custom-call(s32[128]{0:T(128)} %dynamic-slice_bitcast_fusion.1.owners, bf16[128,128,128]{2,1,0:T(8,128)(2,1)} %seg.1, bf16[128,8,128]{2,1,0:T(8,128)(2,1)} %pad.6.tails), custom_call_target="tpu_custom_call" | custom-call | flops 134217728 | bytes 8388608 | tf_op jit(solution)/shard_map/pack/pallas_call | solution.py:84
  19.7 0.0 collective-permute-done.1
  19.7 0.0 collective-permute-done.2
  19.7 0.0 collective-permute-done.4
  19.7 0.0 collective-permute-done.5
  19.7 63.6 %all_to_all.10.recv = bf16[128,136,128]{2,1,0:T(8,128)(2,1)} all-to-all(bf16[128,136,128]{2,1,0:T(8,128)(2,1)} %get-tuple-element.12), channel_id=1, replica_groups=mesh['gx'=4,'gy'=4,'gz'=8] {'gx','gy','gz'}, dimensions={0} | all-to-all | bytes 8912896 | tf_op jit(solution)/shard_map/all_to_all | solution.py:369
  83.3 1.9 %fold.1 = bf16[128,136,128]{2,1,0:T(8,128)(2,1)} custom-call(bf16[128,136,128]{2,1,0:T(8,128)(2,1)} %all_to_all.10.recv, bf16[128,136,128]{2,1,0:T(8,128)(2,1)} %get-tuple-element.13.send), custom_call_target="tpu_custom_call", output_to_operand_aliasing={{}: (1, {})} | custom-call | tf_op jit(solution)/shard_map/fold/pallas_call | solution.py:138
  85.2 0.0 copy-start.2
  85.2 0.0 copy-start.1
  85.3 5.9 %all-to-all-start.1 = ((bf16[128,136,128]{2,1,0:T(8,128)(2,1)}), bf16[128,136,128]{2,1,0:T(8,128)(2,1)}, u32[]{:S(2)}, u32[]{:S(2)}) async-start(bf16[128,136,128]{2,1,0:T(8,128)(2,1)} %fold.1), calls=%async_computation.1 | async-start | bytes 8912896 | tf_op jit(solution)/shard_map/all_to_all | solution.py:370
  91.2 0.1 convert_reduce_fusion.arrivals
  91.4 0.1 pad_maximum_fusion
  91.5 0.2 copy.13.ghost_t
  91.7 0.2 multiply_reduce_fusion
  91.9 2.3 %copy-done = bf16[128,136,128]{2,1,0:T(8,128)(2,1)S(1)} copy-done((bf16[128,136,128]{2,1,0:T(8,128)(2,1)S(1)}, bf16[128,136,128]{2,1,0:T(8,128)(2,1)}, u32[]{:S(2)}) %copy-start) | copy-done | bytes 4456472
  94.2 30.0 %forces.2.rest_0_ = bf16[128,2,128,128]{3,2,1,0:T(8,128)(2,1)} custom-call(s32[128]{0:T(128)S(1)} %convert_reduce_fusion.arrivals, bf16[128,136,128]{2,1,0:T(8,128)(2,1)S(1)} %copy-done, bf16[256,768]{1,0:T(8,128)(2,1)S(1)} %copy.13.ghost_t, bf16[768,256]{1,0:T(8,128)(2,1)S(1)} %concatenate.11.ghost_aug, f32[1,768]{1,0:T(1,128)S(1)} %add.32.ghost_sq), custom_call_target="tpu_custom_call" | custom-call | flops 11274289152 | bytes 8388608 | tf_op jit(solution)/shard_map/forces/pallas_call | solution.py:316
  124.2 22.7 %all-to-all-done.1.recv = bf16[128,136,128]{2,1,0:T(8,128)(2,1)} async-done(((bf16[128,136,128]{2,1,0:T(8,128)(2,1)}), bf16[128,136,128]{2,1,0:T(8,128)(2,1)}, u32[]{:S(2)}, u32[]{:S(2)}) %all-to-all-start.1) | async-done | bytes 4456480 | tf_op jit(solution)/shard_map/all_to_all | solution.py:370
  146.9 2.5 %cuts.1 = f32[8,128]{1,0:T(8,128)} custom-call(bf16[128,136,128]{2,1,0:T(8,128)(2,1)} %all-to-all-done.1.recv), custom_call_target="tpu_custom_call" | custom-call | tf_op jit(solution)/shard_map/cuts/pallas_call | solution.py:198
  149.4 1.3 slice_reduce_fusion
  150.7 31.6 %forces.3 = bf16[128,2,128,128]{3,2,1,0:T(8,128)(2,1)} custom-call(s32[128]{0:T(128)S(1)} %convert_reduce_fusion.arrivals, bf16[128,136,128]{2,1,0:T(8,128)(2,1)} %all-to-all-done.1.recv, bf16[256,768]{1,0:T(8,128)(2,1)S(1)} %copy.13.ghost_t, bf16[768,256]{1,0:T(8,128)(2,1)S(1)} %concatenate.11.ghost_aug, ...), custom_call_target="tpu_custom_call", output_to_operand_aliasing={{}: (5, {})} | custom-call | flops 11274289152 | bytes 8388608 | tf_op jit(solution)/shard_map/forces/pallas_call | solution.py:316
  (16 shorter events, 0.2 us)
Async XLA Ops:
  2.0 10.2 %collective-permute-start = (bf16[128,128]{1,0:T(8,128)(2,1)S(1)}, bf16[128,128]{1,0:T(8,128)(2,1)S(1)}, u32[]{:S(2)}, u32[]{:S(2)}) collective-permute-start(bf16[128,128]{1,0:T(8,128)(2,1)S(1)} %dynamic-slice_bitcast_fusion), channel_id=1, source_target_pairs={{0,32},{32,64},{64,96},{96,0},{1,33},{33,65},{65,97},{97,1},{2,34}... | collective-permute-start | bytes 98312 | tf_op jit(solution)/shard_map/ppermute | solution.py:355
  4.1 15.6 %collective-permute-start.1 = (bf16[128,128]{1,0:T(8,128)(2,1)S(1)}, bf16[128,128]{1,0:T(8,128)(2,1)S(1)}, u32[]{:S(2)}, u32[]{:S(2)}) collective-permute-start(bf16[128,128]{1,0:T(8,128)(2,1)S(1)} %dynamic-slice_bitcast_fusion), channel_id=1, source_target_pairs={{0,96},{32,0},{64,32},{96,64},{1,97},{33,1},{65,33},{97,65},{2,98}... | collective-permute-start | bytes 98312 | tf_op jit(solution)/shard_map/ppermute | solution.py:356
  5.3 14.3 %collective-permute-start.2 = (bf16[128,128]{1,0:T(8,128)(2,1)S(1)}, bf16[128,128]{1,0:T(8,128)(2,1)S(1)}, u32[]{:S(2)}, u32[]{:S(2)}) collective-permute-start(bf16[128,128]{1,0:T(8,128)(2,1)S(1)} %dynamic-slice_bitcast_fusion), channel_id=1, source_target_pairs={{0,8},{8,16},{16,24},{24,0},{1,9},{9,17},{17,25},{25,1},{2,10},{10... | collective-permute-start | bytes 98312 | tf_op jit(solution)/shard_map/ppermute | solution.py:355
  6.8 12.9 %collective-permute-start.3 = (bf16[128,128]{1,0:T(8,128)(2,1)S(1)}, bf16[128,128]{1,0:T(8,128)(2,1)S(1)}, u32[]{:S(2)}, u32[]{:S(2)}) collective-permute-start(bf16[128,128]{1,0:T(8,128)(2,1)S(1)} %dynamic-slice_bitcast_fusion), channel_id=1, source_target_pairs={{0,24},{8,0},{16,8},{24,16},{1,25},{9,1},{17,9},{25,17},{2,26},{10... | collective-permute-start | bytes 98312 | tf_op jit(solution)/shard_map/ppermute | solution.py:356
  8.3 11.4 %collective-permute-start.4 = (bf16[128,128]{1,0:T(8,128)(2,1)S(1)}, bf16[128,128]{1,0:T(8,128)(2,1)S(1)}, u32[]{:S(2)}, u32[]{:S(2)}) collective-permute-start(bf16[128,128]{1,0:T(8,128)(2,1)S(1)} %dynamic-slice_bitcast_fusion), channel_id=1, source_target_pairs={{0,1},{1,2},{2,3},{3,4},{4,5},{5,6},{6,7},{7,0},{8,9},{9,10},{10,1... | collective-permute-start | bytes 98312 | tf_op jit(solution)/shard_map/ppermute | solution.py:355
  12.3 7.4 %collective-permute-start.5 = (bf16[128,128]{1,0:T(8,128)(2,1)S(1)}, bf16[128,128]{1,0:T(8,128)(2,1)S(1)}, u32[]{:S(2)}, u32[]{:S(2)}) collective-permute-start(bf16[128,128]{1,0:T(8,128)(2,1)S(1)} %dynamic-slice_bitcast_fusion), channel_id=1, source_target_pairs={{0,7},{1,0},{2,1},{3,2},{4,3},{5,4},{6,5},{7,6},{8,15},{9,8},{10,9... | collective-permute-start | bytes 98312 | tf_op jit(solution)/shard_map/ppermute | solution.py:356
  85.2 5.9 %copy-start.2 = (bf16[128]{0:T(256)(128)(2,1)S(1)}, bf16[128]{0:T(256)(128)(2,1)}, u32[]{:S(2)}) copy-start(bf16[128]{0:T(256)(128)(2,1)} %constant.42.clone) | copy-start | bytes 772
  85.2 6.0 %copy-start.1 = (s32[16384,1]{0,1:T(1,128)S(1)}, s32[16384,1]{0,1:T(1,128)}, u32[]{:S(2)}) copy-start(s32[16384,1]{0,1:T(1,128)} %param.6) | copy-start | bytes 196612
  85.3 61.6 %all-to-all-start.1 = ((bf16[128,136,128]{2,1,0:T(8,128)(2,1)}), bf16[128,136,128]{2,1,0:T(8,128)(2,1)}, u32[]{:S(2)}, u32[]{:S(2)}) async-start(bf16[128,136,128]{2,1,0:T(8,128)(2,1)} %fold.1), calls=%async_computation.1 | async-start | bytes 8912896 | tf_op jit(solution)/shard_map/all_to_all | solution.py:370
  91.9 2.3 %copy-start = (bf16[128,136,128]{2,1,0:T(8,128)(2,1)S(1)}, bf16[128,136,128]{2,1,0:T(8,128)(2,1)}, u32[]{:S(2)}) copy-start(bf16[128,136,128]{2,1,0:T(8,128)(2,1)} %all_to_all.10.recv) | copy-start | bytes 13369348
